TPU v7x, 256 devices: a whole 4x4x8 slice. The times are simulated.
256 devices in a mesh: band: 16 (over z, y_lo), grid: 16 (over x, y_hi, core).
Axes of the slice: x: 4, y: 4 (y_hi: 2, y_lo: 2; y = y_hi * 2 + y_lo), z: 8, core: 2. Of those that a mesh axis runs over, the one named last changes fastest.
Arguments:
- orbitals: bfloat16 [16, 128, 128, 128], P('band', 'grid'), may hold values from -3 to 3
- trial_vectors: bfloat16 [2, 16, 128, 128, 128], P(None, 'band', 'grid'), may hold values from -6 to 6
- alda_kernel: float32 [128, 128, 128], P('grid'), may hold values from -2 to -0.5
- local_potential: float32 [128, 128, 128], P('grid'), may hold values from -2 to 1
- band_energies: float32 [16], P('band'), may hold values from -1.5 to -0.2
Outputs:
- sigma_real: float32 [2, 16, 128, 128, 128], P(None, 'band', 'grid')
- sigma_imag: float32 [2, 16, 128, 128, 128], P(None, 'band', 'grid')
All inputs are finite; a program needn't handle non-finite values.
Results may differ from a plain program's by a relative error of at most 0.0003.
Values sent between devices are 32-bit elements; how exact they have to be, the bound alone decides.
No kernel may reach another device: no remote copies, remote signals or barrier semaphores. Data moves between devices by JAX's collectives and lax.ppermute only.
A program may use at most 64 MiB of HBM per device.

v0:
```python
import functools
import math

import jax
import jax.numpy as jnp
import numpy as np
from jax import lax
from jax.experimental import pallas as pl
from jax.experimental.pallas import tpu as pltpu
from jax.sharding import PartitionSpec as P


box_length = 30.0
NARROW = jnp.bfloat16
WIDE = jnp.float32
ROWS = 8
GRANT = 20 * 2**20
WIDE_GRANT = 60 * 2**20


def halves(table):
    high = table.astype(np.float32).astype(jnp.bfloat16)
    low = (table - high.astype(np.float64)).astype(np.float32).astype(jnp.bfloat16)
    return np.stack([high, low])


@functools.cache
def make_tables(length):
    wrapped = np.outer(np.arange(length), np.arange(length)) % length
    angles = wrapped.astype(np.float64) * (2.0 * math.pi / length)
    cosine, sine = np.cos(angles), np.sin(angles)
    return {
        "down": halves(np.block([[cosine, sine], [-sine, cosine]])),
        "up": halves(np.block([[cosine, -sine], [sine, cosine]])),
        "last": halves(np.block([[cosine, -sine], [sine, cosine]]) * float(length) ** -1.5),
    }


def split(value):
    high = value.astype(NARROW)
    return high, (value - high.astype(WIDE)).astype(NARROW)


def mul(left, right):
    return lax.dot_general(left, right, (((1,), (0,)), ((), ())), preferred_element_type=WIDE)


def product(left, right):
    left_high, left_low = left
    right_high, right_low = right
    return mul(left_high, right_high) + mul(left_low, right_high) + mul(left_high, right_low)


def pair(ref):
    return ref[0], ref[1]


def swap_blocks(value):
    rows, columns = value.shape[0] // 2, value.shape[1] // 2
    left = jnp.concatenate([value[:rows, :columns], value[rows:, :columns]], axis=1)
    right = jnp.concatenate([value[:rows, columns:], value[rows:, columns:]], axis=1)
    return jnp.concatenate([left, right], axis=0)


def parts_down(value):
    half = value.shape[1] // 2
    return jnp.concatenate([value[:, :half], value[:, half:]], axis=0)


def parts_across(value):
    half = value.shape[0] // 2
    return jnp.concatenate([value[:half], value[half:]], axis=1)


def density_kernel(me_ref, orbital_in, trial_in, up_in, down_in, *refs):
    (
        kept_hbm, near_hbm, out_hbm, orbital_ref, trial_ref, up_ref, down_ref, mixed_ref, out_ref,
        table_sems, row_sems, out_sems,
    ) = refs
    me = me_ref[0]
    length = orbital_ref.shape[2]
    parts, share = out_ref.shape[0], out_ref.shape[3]
    half = orbital_ref.shape[1] // 2
    tables = [
        pltpu.make_async_copy(up_in, up_ref, table_sems.at[0]),
        pltpu.make_async_copy(down_in, down_ref, table_sems.at[1]),
    ]
    rows = [pl.ds(i * half, half) for i in range(2)]
    orbitals, trials = [], []
    for i in range(2):
        part = (slice(None), rows[i])
        orbitals.append(
            pltpu.make_async_copy(orbital_in.at[part], orbital_ref.at[part], row_sems.at[i, 0])
        )
        part = (slice(None), slice(None), rows[i])
        trials.append(
            pltpu.make_async_copy(trial_in.at[part], trial_ref.at[part], row_sems.at[i, 1])
        )
    outs = [
        [
            pltpu.make_async_copy(mixed_ref.at[1], near_hbm, out_sems.at[1]),
            pltpu.make_async_copy(mixed_ref.at[0], kept_hbm, out_sems.at[0]),
        ],
        [pltpu.make_async_copy(out_ref, out_hbm, out_sems.at[2])],
    ]
    for copy in (tables[0], orbitals[0], trials[0], tables[1], orbitals[1], trials[1]):
        copy.start()
    for copy in tables:
        copy.wait()
    for i in range(2):
        orbitals[i].wait()
        trials[i].wait()
        values = []
        for x in range(half):
            orbital = 2.0 * orbital_ref[0, i * half + x].astype(WIDE)
            values.append(
                jnp.concatenate(
                    [trial_ref[k, 0, i * half + x].astype(WIDE) * orbital for k in range(2)], axis=1
                )
            )
        turned = product(split(jnp.concatenate(values, axis=0)), pair(up_ref))
        columns = [parts_down(turned[x * length : (x + 1) * length]) for x in range(half)]
        turned = product(pair(down_ref), split(jnp.concatenate(columns, axis=1)))
        for x in range(half):
            for part in range(2):
                block = turned[part * length : (part + 1) * length, x * length : (x + 1) * length]
                if i == 1:
                    out_ref[:, part, x] = block.reshape(parts, share, length)
                    continue
                for n in range(parts):
                    tile = block[n * share : (n + 1) * share]
                    mixed_ref[(n ^ me) & 1, (n ^ me) >> 1, part, x] = tile
        for copy in outs[i]:
            copy.start()
    for copy in outs[0] + outs[1]:
        copy.wait()


def share_kernel(pieces_ref, *refs):
    *near_refs, share_ref, out_ref = refs
    first = near_refs[0][...]
    for ref in near_refs[1:]:
        first = first + ref[...]
    second = pieces_ref[0]
    for i in range(1, pieces_ref.shape[0]):
        second = second + pieces_ref[i]
    rows = first.shape[0] // 2
    for part in range(2):
        held = slice(part * rows, (part + 1) * rows)
        share_ref[2 * part * rows : (2 * part + 1) * rows, :] = first[held]
        share_ref[(2 * part + 1) * rows : 2 * (part + 1) * rows, :] = second[held]
    copies, rows, _ = out_ref.shape
    share = rows // 2
    for b in range(share):
        block = share_ref[pl.ds(b, rows, stride=share), :]
        for i in range(copies // share):
            out_ref[b * (copies // share) + i] = block


def line_kernel(pieces_ref, kernel_ref, down_ref, up_ref, out_ref):
    parts, rows, length = pieces_ref.shape
    share = rows // 2
    columns = jnp.concatenate(
        [pieces_ref[:, :share, :].reshape(length, length), pieces_ref[:, share:, :].reshape(length, length)],
        axis=0,
    )
    turned = product(pair(down_ref), split(columns))
    kernel = kernel_ref[...]
    turned = turned * jnp.concatenate([kernel, kernel], axis=0)
    out_ref[...] = product(pair(up_ref), split(turned)).reshape(parts, share, length)


def spread_kernel(pieces_ref, out_ref):
    share = pieces_ref.shape[0] // out_ref.shape[0]
    for part in range(2):
        for x in range(share):
            block = pieces_ref[pl.ds(part * share + x, share, stride=2 * share), :]
            rows = pl.ds((part * share + x) * share, share)
            for i in range(out_ref.shape[0]):
                out_ref[i, rows, :] = block


def back(blocks, up_ref, down_ref, length):
    turned = product(pair(up_ref), split(blocks))
    rows = turned.shape[1] // length
    points = [parts_across(turned[:, x * length : (x + 1) * length]) for x in range(rows)]
    return product(split(jnp.concatenate(points, axis=0)), pair(down_ref))


def base_kernel(
    me_ref, energy_ref, near_ref, far_ref, orbital_ref, trial_ref, alda_ref, local_ref,
    up_ref, down_ref, out_ref,
):
    length = orbital_ref.shape[2]
    parts = 2 * near_ref.shape[0]
    me = me_ref[0]
    energy = energy_ref[0]
    even = (me & 1) == 0
    scale = 1.0 / float(length * length)
    rows = orbital_ref.shape[1]
    columns = []
    for x in range(rows):
        tiles = []
        for part in range(2):
            for half in range(parts // 2):
                slot = half ^ (me >> 1)
                near = near_ref[slot, part, x]
                far = far_ref[slot, part, x]
                tiles.append(jnp.where(even, near, far))
                tiles.append(jnp.where(even, far, near))
        columns.append(jnp.concatenate(tiles, axis=0))
    value = back(jnp.concatenate(columns, axis=1), up_ref, down_ref, length)
    for x in range(rows):
        factor = orbital_ref[0, x].astype(WIDE) * (alda_ref[x] * scale)
        weight = local_ref[x] - energy
        for k in range(2):
            block = value[x * length : (x + 1) * length, k * length : (k + 1) * length]
            out_ref[k, x] = block * factor + weight * trial_ref[k, 0, x].astype(WIDE)


def field_kernel(potential_ref, orbital_ref, base_ref, up_ref, down_ref, out_ref):
    length = orbital_ref.shape[2]
    parts = potential_ref.shape[0]
    rows = orbital_ref.shape[1]
    columns = []
    for x in range(rows):
        columns.append(
            jnp.concatenate(
                [potential_ref[:, part, x].reshape(length, length) for part in range(2)], axis=0
            )
        )
    value = back(jnp.concatenate(columns, axis=1), up_ref, down_ref, length)
    fields = []
    for x in range(rows):
        orbital = orbital_ref[0, x].astype(WIDE)
        for k in range(2):
            block = value[x * length : (x + 1) * length, k * length : (k + 1) * length]
            fields.append(block * orbital + base_ref[k, x])
    table = (up_ref[0, :length, :], up_ref[1, :length, :])
    turned = product(split(jnp.concatenate(fields, axis=0)), table)
    for x in range(rows):
        points = swap_blocks(turned[2 * x * length : 2 * (x + 1) * length])
        waves = product(pair(down_ref), split(points))
        for k in range(2):
            for part in range(2):
                block = waves[part * length : (part + 1) * length, k * length : (k + 1) * length]
                out_ref[:, k, part, x] = block.reshape(parts, length // parts, length)


def final_kernel(pieces_ref, x_ref, real_ref, imag_ref):
    length = real_ref.shape[-1]
    share = real_ref.shape[2]
    table = pair(x_ref)
    for k in range(2):
        for b in range(share):
            parts = []
            for part in range(2):
                start = (k * 2 + part) * share * share + b
                block = pieces_ref[:, pl.ds(start, share, stride=share), :]
                parts.append(block.reshape(length, length))
            turned = product(split(jnp.concatenate(parts, axis=0).T), table)
            real_ref[k, 0, b] = turned[:, :length]
            imag_ref[k, 0, b] = turned[:, length:]


def signed(positions, length):
    return jnp.where(2 * positions < length, positions, positions - length).astype(WIDE)


def line_coulomb(b, length):
    a = lax.broadcasted_iota(jnp.int32, (length, length), 0)
    c = lax.broadcasted_iota(jnp.int32, (length, length), 1)
    squared = signed(a, length) ** 2 + signed(b, length) ** 2 + signed(c, length) ** 2
    scaled = box_length**2 / math.pi / jnp.maximum(squared, 1.0)
    return jnp.where(squared > 0, scaled, 0.0) / float(length**3)


def call(body, shapes, grant=GRANT, **options):
    return pl.pallas_call(
        body,
        out_shape=jax.tree.map(
            lambda s: jax.ShapeDtypeStruct(s, WIDE),
            shapes,
            is_leaf=lambda s: isinstance(s, tuple) and isinstance(s[0], int),
        ),
        compiler_params=pltpu.CompilerParams(vmem_limit_bytes=grant),
        **options,
    )


def exchange(array, axis):
    return lax.all_to_all(array, axis, split_axis=0, concat_axis=0, tiled=True)


def partner(array, mask):
    return lax.ppermute(array, "band", [(i, i ^ mask) for i in range(lax.axis_size("band"))])


def per_device(orbitals, trials, alda_kernel, local_potential, band_energies):
    length = orbitals.shape[2]
    parts = lax.axis_size("band")
    share = length // parts
    points = share * share
    tables = {name: jnp.asarray(table) for name, table in make_tables(length).items()}
    me = lax.axis_index("band")
    place = lax.axis_index("grid")
    copies = parts // share
    kernel = line_coulomb(me * share + place // copies, length)
    own_up = lax.dynamic_slice_in_dim(tables["up"], (place % copies) * length, length, 1)

    scalar = pl.BlockSpec(memory_space=pltpu.SMEM)
    orbital_block = pl.BlockSpec((1, ROWS, length, length), lambda i: (0, i, 0, 0))
    trial_block = pl.BlockSpec((2, 1, ROWS, length, length), lambda i: (0, 0, i, 0, 0))
    table_block = pl.BlockSpec((2, 2 * length, 2 * length), lambda i: (0, 0, 0))
    share_block = pl.BlockSpec((parts, 2, ROWS, share, length), lambda i: (0, 0, i, 0, 0))
    half_block = pl.BlockSpec((parts // 2, 2, ROWS, share, length), lambda i: (0, 0, i, 0, 0))
    local_block = pl.BlockSpec((ROWS, length, length), lambda i: (i, 0, 0))
    base_block = pl.BlockSpec((2, ROWS, length, length), lambda i: (0, i, 0, 0))
    steps = (share // ROWS,)

    held = pl.BlockSpec(memory_space=pltpu.HBM)
    half = share // 2
    some = (parts // 2, 2, half, share, length)
    kept, near, pieces = call(
        density_kernel,
        [some, some, (parts, 2, half, share, length)],
        grant=WIDE_GRANT,
        in_specs=[scalar] + [held] * 4,
        out_specs=[held] * 3,
        scratch_shapes=[
            pltpu.VMEM(orbitals.shape, NARROW),
            pltpu.VMEM(trials.shape, NARROW),
            pltpu.VMEM(tables["up"].shape, NARROW),
            pltpu.VMEM(tables["down"].shape, NARROW),
            pltpu.VMEM((2, *some), WIDE),
            pltpu.VMEM((parts, 2, half, share, length), WIDE),
            pltpu.SemaphoreType.DMA((2,)),
            pltpu.SemaphoreType.DMA((2, 2)),
            pltpu.SemaphoreType.DMA((3,)),
        ],
    )(me.reshape(1), orbitals, trials, tables["up"], tables["down"])
    near = partner(near.reshape(parts // 2, points, length), 1)
    near = near + kept.reshape(parts // 2, points, length)
    near = [near[0]] + [partner(near[i], 2 * i) for i in range(1, parts // 2)]
    pieces = exchange(pieces.reshape(parts, points, length), "band")
    spectrum, lines = call(
        share_kernel, [(2 * points, length), (parts, 2 * share, length)]
    )(pieces, *near)
    lines = exchange(lines, "grid")
    held = {0: spectrum}
    for mask in (2, 4, 8):
        held[mask] = partner(spectrum, mask)
    lines = call(line_kernel, (parts, share, length))(
        lines, kernel, tables["down"], own_up
    )
    _, held[2], held[4], held[8] = lax.optimization_barrier((lines, held[2], held[4], held[8]))
    lines = exchange(lines, "grid").reshape(parts * share, length)
    both = partner(jnp.stack([held[4], held[8]]), 2)
    held[6], held[10] = both[0], both[1]
    held[12] = partner(held[8], 4)
    held[14] = partner(spectrum, 14)
    away = {}
    for masks in ((0, 2, 4, 8), (6, 10, 12, 14)):
        group = partner(jnp.stack([held[mask] for mask in masks]), 1)
        for i, mask in enumerate(masks):
            away[mask] = group[i]
    near = jnp.stack([held[mask] for mask in range(0, parts, 2)])
    far = jnp.stack([away[mask] for mask in range(0, parts, 2)])
    potential = call(spread_kernel, (parts, 2 * points, length))(lines)
    potential = exchange(potential, "band").reshape(parts, 2, share, share, length)
    base = call(
        base_kernel,
        (2, share, length, length),
        grid=steps,
        in_specs=[
            scalar, scalar, half_block, half_block, orbital_block, trial_block,
            local_block, local_block, table_block, table_block,
        ],
        out_specs=base_block,
    )(
        me.reshape(1),
        band_energies,
        near.reshape(parts // 2, 2, share, share, length),
        far.reshape(parts // 2, 2, share, share, length),
        orbitals,
        trials,
        alda_kernel,
        local_potential,
        tables["up"],
        tables["down"],
    )
    fields = call(
        field_kernel,
        (parts, 2, 2, share, share, length),
        grid=steps,
        in_specs=[share_block, orbital_block, base_block, table_block, table_block],
        out_specs=pl.BlockSpec(
            (parts, 2, 2, ROWS, share, length), lambda i: (0, 0, 0, i, 0, 0)
        ),
    )(potential, orbitals, base, tables["up"], tables["down"])
    received = exchange(fields.reshape(parts, 4 * points, length), "grid")
    shape = (2, 1, share, length, length)
    return tuple(call(final_kernel, [shape, shape])(received, tables["last"]))


def solution(mesh):
    placed = (
        P("band", "grid", None, None),
        P(None, "band", "grid", None, None),
        P("grid", None, None),
        P("grid", None, None),
        P("band"),
    )

    return jax.shard_map(
        per_device,
        mesh=mesh,
        in_specs=placed,
        out_specs=(P(None, "band", "grid", None, None), P(None, "band", "grid", None, None)),
        check_vma=False,
    )
```

profile of v0, /device:TPU:1, one launch (start us, length us, event | category | flops | bytes accessed | tf_op | source)
XLA Modules:
  0.0 167.8 jit_solution(15862094304337165115)
XLA Ops:
  0.6 4.2 %shard_map.95 = (f32[8,2,4,8,128]{4,3,2,1,0:T(8,128)}, f32[8,2,4,8,128]{4,3,2,1,0:T(8,128)}, f32[16,2,4,8,128]{4,3,2,1,0:T(8,128)}) custom-call(s32[1]{0:T(128)} %bitcast.me_ref, bf16[1,8,128,128]{3,2,1,0:T(8,128)(2,1)} %orbital_ref.3, bf16[2,1,8,128,128]{4,3,2,1,0:T(8,128)(2,1)} %trial_ref.1, bf16[2,256,256]{2,1,0:T(8,128)(2,1)} %constant.61.clone.up_in.up_ref, ...), custom_call_target="tpu_custom_call" | custom-call | tf_op jit(solution)/shard_map/pallas_call | solution.py:324
  4.8 10.3 %all-to-all-start = ((f32[16,64,128]{2,1,0:T(8,128)}), f32[16,64,128]{2,1,0:T(8,128)S(1)}, u32[]{:S(2)}, u32[]{:S(2)}) async-start(f32[16,64,128]{2,1,0:T(8,128)} %bitcast.51), calls=%async_computation | async-start | bytes 1048576 | tf_op jit(solution)/shard_map/all_to_all | solution.py:292
  15.1 1.4 collective-permute-start
  16.5 6.7 %collective-permute-done = f32[8,64,128]{2,1,0:T(8,128)S(1)} collective-permute-done((f32[8,64,128]{2,1,0:T(8,128)}, f32[8,64,128]{2,1,0:T(8,128)S(1)}, u32[]{:S(2)}, u32[]{:S(2)}) %collective-permute-start) | collective-permute-done | bytes 262176 | tf_op jit(solution)/shard_map/ppermute | solution.py:296
  24.2 3.5 %collective-permute-start.7 = (f32[64,128]{1,0:T(8,128)S(1)}, f32[64,128]{1,0:T(8,128)S(1)}, u32[]{:S(2)}, u32[]{:S(2)}) collective-permute-start(f32[64,128]{1,0:T(8,128)S(1)} %get-tuple-element.18), channel_id=1, source_target_pairs={{0,224},{16,240},{32,192},{48,208},{64,160},{80,176},{96,128},{112... | collective-permute-start | bytes 98312 | tf_op jit(solution)/shard_map/ppermute | solution.py:296
  27.7 1.8 %collective-permute-start.6 = (f32[64,128]{1,0:T(8,128)S(1)}, f32[64,128]{1,0:T(8,128)S(1)}, u32[]{:S(2)}, u32[]{:S(2)}) collective-permute-start(f32[64,128]{1,0:T(8,128)S(1)} %get-tuple-element.19), channel_id=1, source_target_pairs={{0,192},{16,208},{32,224},{48,240},{64,128},{80,144},{96,160},{112... | collective-permute-start | bytes 98312 | tf_op jit(solution)/shard_map/ppermute | solution.py:296
  29.5 5.4 %collective-permute-start.5 = (f32[64,128]{1,0:T(8,128)S(1)}, f32[64,128]{1,0:T(8,128)S(1)}, u32[]{:S(2)}, u32[]{:S(2)}) collective-permute-start(f32[64,128]{1,0:T(8,128)S(1)} %get-tuple-element.20), channel_id=1, source_target_pairs={{0,160},{16,176},{32,128},{48,144},{64,224},{80,240},{96,192},{112... | collective-permute-start | bytes 98312 | tf_op jit(solution)/shard_map/ppermute | solution.py:296
  34.9 3.1 %collective-permute-start.3 = (f32[64,128]{1,0:T(8,128)S(1)}, f32[64,128]{1,0:T(8,128)S(1)}, u32[]{:S(2)}, u32[]{:S(2)}) collective-permute-start(f32[64,128]{1,0:T(8,128)S(1)} %get-tuple-element.22), channel_id=1, source_target_pairs={{0,96},{16,112},{32,64},{48,80},{64,32},{80,48},{96,0},{112,16},{1... | collective-permute-start | bytes 98312 | tf_op jit(solution)/shard_map/ppermute | solution.py:296
  38.5 3.4 %collective-permute-done.4.refs_4_ = f32[64,128]{1,0:T(8,128)S(1)} collective-permute-done((f32[64,128]{1,0:T(8,128)S(1)}, f32[64,128]{1,0:T(8,128)S(1)}, u32[]{:S(2)}, u32[]{:S(2)}) %collective-permute-start.4) | collective-permute-done | bytes 32800 | tf_op jit(solution)/shard_map/ppermute | solution.py:296
  42.6 12.1 %all-to-all-start.1 = ((f32[16,16,128]{2,1,0:T(8,128)}), f32[16,16,128]{2,1,0:T(8,128)S(1)}, u32[]{:S(2)}, u32[]{:S(2)}) async-start(f32[16,16,128]{2,1,0:T(8,128)} %get-tuple-element.13), calls=%async_computation.1 | async-start | bytes 262144 | tf_op jit(solution)/shard_map/all_to_all | solution.py:292
  54.9 7.5 %all-to-all-done.1.pieces_ref = f32[16,16,128]{2,1,0:T(8,128)S(1)} async-done(((f32[16,16,128]{2,1,0:T(8,128)}), f32[16,16,128]{2,1,0:T(8,128)S(1)}, u32[]{:S(2)}, u32[]{:S(2)}) %all-to-all-start.1) | async-done | bytes 131104 | tf_op jit(solution)/shard_map/all_to_all | solution.py:292
  62.9 10.3 %all_to_all.25 = f32[16,8,128]{2,1,0:T(8,128)S(1)} all-to-all(f32[16,8,128]{2,1,0:T(8,128)S(1)} %shard_map.97), channel_id=1, replica_groups=mesh['band'=16,'grid'=16] {'grid'}, dimensions={0} | all-to-all | bytes 131072 | tf_op jit(solution)/shard_map/all_to_all | solution.py:292
  74.2 6.0 %all-to-all-start.3 = ((f32[16,128,128]{2,1,0:T(8,128)}), f32[16,128,128]{2,1,0:T(8,128)S(1)}, u32[]{:S(2)}, u32[]{:S(2)}) async-start(f32[16,128,128]{2,1,0:T(8,128)} %shard_map.98), calls=%async_computation.3 | async-start | bytes 2097152 | tf_op jit(solution)/shard_map/all_to_all | solution.py:292
  80.9 2.7 %collective-permute-start.13 = (f32[128,128]{1,0:T(8,128)S(1)}, f32[128,128]{1,0:T(8,128)S(1)}, u32[]{:S(2)}, u32[]{:S(2)}) collective-permute-start(f32[128,128]{1,0:T(8,128)S(1)} %get-tuple-element.14), channel_id=1, source_target_pairs={{0,224},{16,240},{32,192},{48,208},{64,160},{80,176},{96,128},{112... | collective-permute-start | bytes 196616 | tf_op jit(solution)/shard_map/ppermute | solution.py:296
  83.5 3.0 %collective-permute-start.10 = (f32[128,128]{1,0:T(8,128)S(1)}, f32[128,128]{1,0:T(8,128)S(1)}, u32[]{:S(2)}, u32[]{:S(2)}) collective-permute-start(f32[128,128]{1,0:T(8,128)S(1)} %get-tuple-element.14), channel_id=1, source_target_pairs={{0,128},{16,144},{32,160},{48,176},{64,192},{80,208},{96,224},{112... | collective-permute-start | bytes 196616 | tf_op jit(solution)/shard_map/ppermute | solution.py:296
  86.5 1.2 collective-permute-start.9
  87.7 22.7 %collective-permute-done.10 = f32[128,128]{1,0:T(8,128)S(1)} collective-permute-done((f32[128,128]{1,0:T(8,128)S(1)}, f32[128,128]{1,0:T(8,128)S(1)}, u32[]{:S(2)}, u32[]{:S(2)}) %collective-permute-start.10) | collective-permute-done | bytes 65568 | tf_op jit(solution)/shard_map/ppermute | solution.py:296
  110.4 1.2 collective-permute-done.8
  111.6 2.5 %collective-permute-start.12 = (f32[128,128]{1,0:T(8,128)S(1)}, f32[128,128]{1,0:T(8,128)S(1)}, u32[]{:S(2)}, u32[]{:S(2)}) collective-permute-start(f32[128,128]{1,0:T(8,128)S(1)} %collective-permute-done.10), channel_id=1, source_target_pairs={{0,64},{16,80},{32,96},{48,112},{64,0},{80,16},{96,32},{112,48},{1... | collective-permute-start | bytes 196616 | tf_op jit(solution)/shard_map/ppermute | solution.py:296
  115.9 2.6 %collective-permute-done.11 = f32[2,128,128]{2,1,0:T(8,128)S(1)} collective-permute-done((f32[2,128,128]{2,1,0:T(8,128)S(1)}, f32[2,128,128]{2,1,0:T(8,128)S(1)}, u32[]{:S(2)}, u32[]{:S(2)}) %collective-permute-start.11) | collective-permute-done | bytes 131104 | tf_op jit(solution)/shard_map/ppermute | solution.py:296
  120.7 6.1 %collective-permute-done.15 = f32[4,128,128]{2,1,0:T(8,128)S(1)} collective-permute-done((f32[4,128,128]{2,1,0:T(8,128)S(1)}, f32[4,128,128]{2,1,0:T(8,128)S(1)}, u32[]{:S(2)}, u32[]{:S(2)}) %collective-permute-start.15) | collective-permute-done | bytes 262176 | tf_op jit(solution)/shard_map/ppermute | solution.py:296
  128.0 3.8 %shard_map.100 = f32[16,2,2,8,8,128]{5,4,3,2,1,0:T(8,128)S(1)} custom-call(f32[16,2,8,8,128]{4,3,2,1,0:T(8,128)S(1)} %bitcast.40, bf16[1,8,128,128]{3,2,1,0:T(8,128)(2,1)S(1)} %copy-done.2, f32[2,8,128,128]{3,2,1,0:T(8,128)S(1)} %shard_map.99.base_ref, bf16[2,256,256]{2,1,0:T(8,128)(2,1)S(1)} %copy-done.1, bf16[2,256,256]{2,1,0:T(8,128)(2,1)S(1)} %copy-done), custom_call_target="tpu_custom_call" | custom-call | tf_op jit(solution)/shard_map/pallas_call | solution.py:392
  131.8 33.6 %all_to_all.26.pieces_ref = f32[16,256,128]{2,1,0:T(8,128)S(1)} all-to-all(f32[16,256,128]{2,1,0:T(8,128)S(1)} %bitcast.39), channel_id=1, replica_groups=mesh['band'=16,'grid'=16] {'grid'}, dimensions={0} | all-to-all | bytes 4194304 | tf_op jit(solution)/shard_map/all_to_all | solution.py:292
  165.4 2.4 %shard_map.101 = (f32[2,1,8,128,128]{4,3,2,1,0:T(8,128)}, f32[2,1,8,128,128]{4,3,2,1,0:T(8,128)}) custom-call(f32[16,256,128]{2,1,0:T(8,128)S(1)} %all_to_all.26.pieces_ref, bf16[2,256,256]{2,1,0:T(8,128)(2,1)S(1)} %copy-done.6), custom_call_target="tpu_custom_call" | custom-call | tf_op jit(solution)/shard_map/pallas_call | solution.py:403
  (60 shorter events, 9.1 us)
Async XLA Ops:
  4.8 50.1 %copy-start.1 = (bf16[2,256,256]{2,1,0:T(8,128)(2,1)S(1)}, bf16[2,256,256]{2,1,0:T(8,128)(2,1)}, u32[]{:S(2)}) copy-start(bf16[2,256,256]{2,1,0:T(8,128)(2,1)} %constant.61.clone.up_in.up_ref) | copy-start | bytes 786436
  4.8 57.6 %copy-start = (bf16[2,256,256]{2,1,0:T(8,128)(2,1)S(1)}, bf16[2,256,256]{2,1,0:T(8,128)(2,1)}, u32[]{:S(2)}) copy-start(bf16[2,256,256]{2,1,0:T(8,128)(2,1)} %constant.60.clone.down_in.down_ref) | copy-start | bytes 786436
  4.8 37.0 %all-to-all-start = ((f32[16,64,128]{2,1,0:T(8,128)}), f32[16,64,128]{2,1,0:T(8,128)S(1)}, u32[]{:S(2)}, u32[]{:S(2)}) async-start(f32[16,64,128]{2,1,0:T(8,128)} %bitcast.51), calls=%async_computation | async-start | bytes 1048576 | tf_op jit(solution)/shard_map/all_to_all | solution.py:292
  15.1 8.1 %collective-permute-start = (f32[8,64,128]{2,1,0:T(8,128)}, f32[8,64,128]{2,1,0:T(8,128)S(1)}, u32[]{:S(2)}, u32[]{:S(2)}) collective-permute-start(f32[8,64,128]{2,1,0:T(8,128)} %bitcast.60), channel_id=1, source_target_pairs={{0,16},{16,0},{32,48},{48,32},{64,80},{80,64},{96,112},{112,96},{1... | collective-permute-start | bytes 786440 | tf_op jit(solution)/shard_map/ppermute | solution.py:296
  24.2 13.8 %collective-permute-start.7 = (f32[64,128]{1,0:T(8,128)S(1)}, f32[64,128]{1,0:T(8,128)S(1)}, u32[]{:S(2)}, u32[]{:S(2)}) collective-permute-start(f32[64,128]{1,0:T(8,128)S(1)} %get-tuple-element.18), channel_id=1, source_target_pairs={{0,224},{16,240},{32,192},{48,208},{64,160},{80,176},{96,128},{112... | collective-permute-start | bytes 98312 | tf_op jit(solution)/shard_map/ppermute | solution.py:296
  27.7 10.3 %collective-permute-start.6 = (f32[64,128]{1,0:T(8,128)S(1)}, f32[64,128]{1,0:T(8,128)S(1)}, u32[]{:S(2)}, u32[]{:S(2)}) collective-permute-start(f32[64,128]{1,0:T(8,128)S(1)} %get-tuple-element.19), channel_id=1, source_target_pairs={{0,192},{16,208},{32,224},{48,240},{64,128},{80,144},{96,160},{112... | collective-permute-start | bytes 98312 | tf_op jit(solution)/shard_map/ppermute | solution.py:296
  29.5 9.0 %collective-permute-start.5 = (f32[64,128]{1,0:T(8,128)S(1)}, f32[64,128]{1,0:T(8,128)S(1)}, u32[]{:S(2)}, u32[]{:S(2)}) collective-permute-start(f32[64,128]{1,0:T(8,128)S(1)} %get-tuple-element.20), channel_id=1, source_target_pairs={{0,160},{16,176},{32,128},{48,144},{64,224},{80,240},{96,192},{112... | collective-permute-start | bytes 98312 | tf_op jit(solution)/shard_map/ppermute | solution.py:296
  34.9 6.9 %collective-permute-start.4 = (f32[64,128]{1,0:T(8,128)S(1)}, f32[64,128]{1,0:T(8,128)S(1)}, u32[]{:S(2)}, u32[]{:S(2)}) collective-permute-start(f32[64,128]{1,0:T(8,128)S(1)} %get-tuple-element.21), channel_id=1, source_target_pairs={{0,128},{16,144},{32,160},{48,176},{64,192},{80,208},{96,224},{112... | collective-permute-start | bytes 98312 | tf_op jit(solution)/shard_map/ppermute | solution.py:296
  34.9 6.9 %collective-permute-start.3 = (f32[64,128]{1,0:T(8,128)S(1)}, f32[64,128]{1,0:T(8,128)S(1)}, u32[]{:S(2)}, u32[]{:S(2)}) collective-permute-start(f32[64,128]{1,0:T(8,128)S(1)} %get-tuple-element.22), channel_id=1, source_target_pairs={{0,96},{16,112},{32,64},{48,80},{64,32},{80,48},{96,0},{112,16},{1... | collective-permute-start | bytes 98312 | tf_op jit(solution)/shard_map/ppermute | solution.py:296
  38.0 3.9 %collective-permute-start.2 = (f32[64,128]{1,0:T(8,128)S(1)}, f32[64,128]{1,0:T(8,128)S(1)}, u32[]{:S(2)}, u32[]{:S(2)}) collective-permute-start(f32[64,128]{1,0:T(8,128)S(1)} %get-tuple-element.23), channel_id=1, source_target_pairs={{0,64},{16,80},{32,96},{48,112},{64,0},{80,16},{96,32},{112,48},{1... | collective-permute-start | bytes 98312 | tf_op jit(solution)/shard_map/ppermute | solution.py:296
  38.0 3.9 %collective-permute-start.1 = (f32[64,128]{1,0:T(8,128)S(1)}, f32[64,128]{1,0:T(8,128)S(1)}, u32[]{:S(2)}, u32[]{:S(2)}) collective-permute-start(f32[64,128]{1,0:T(8,128)S(1)} %get-tuple-element.24), channel_id=1, source_target_pairs={{0,32},{16,48},{32,0},{48,16},{64,96},{80,112},{96,64},{112,80},{1... | collective-permute-start | bytes 98312 | tf_op jit(solution)/shard_map/ppermute | solution.py:296
  42.6 19.8 %all-to-all-start.1 = ((f32[16,16,128]{2,1,0:T(8,128)}), f32[16,16,128]{2,1,0:T(8,128)S(1)}, u32[]{:S(2)}, u32[]{:S(2)}) async-start(f32[16,16,128]{2,1,0:T(8,128)} %get-tuple-element.13), calls=%async_computation.1 | async-start | bytes 262144 | tf_op jit(solution)/shard_map/all_to_all | solution.py:292
  74.2 53.8 %all-to-all-start.3 = ((f32[16,128,128]{2,1,0:T(8,128)}), f32[16,128,128]{2,1,0:T(8,128)S(1)}, u32[]{:S(2)}, u32[]{:S(2)}) async-start(f32[16,128,128]{2,1,0:T(8,128)} %shard_map.98), calls=%async_computation.3 | async-start | bytes 2097152 | tf_op jit(solution)/shard_map/all_to_all | solution.py:292
  80.9 34.9 %collective-permute-start.13 = (f32[128,128]{1,0:T(8,128)S(1)}, f32[128,128]{1,0:T(8,128)S(1)}, u32[]{:S(2)}, u32[]{:S(2)}) collective-permute-start(f32[128,128]{1,0:T(8,128)S(1)} %get-tuple-element.14), channel_id=1, source_target_pairs={{0,224},{16,240},{32,192},{48,208},{64,160},{80,176},{96,128},{112... | collective-permute-start | bytes 196616 | tf_op jit(solution)/shard_map/ppermute | solution.py:296
  83.5 26.8 %collective-permute-start.10 = (f32[128,128]{1,0:T(8,128)S(1)}, f32[128,128]{1,0:T(8,128)S(1)}, u32[]{:S(2)}, u32[]{:S(2)}) collective-permute-start(f32[128,128]{1,0:T(8,128)S(1)} %get-tuple-element.14), channel_id=1, source_target_pairs={{0,128},{16,144},{32,160},{48,176},{64,192},{80,208},{96,224},{112... | collective-permute-start | bytes 196616 | tf_op jit(solution)/shard_map/ppermute | solution.py:296
  86.5 23.8 %collective-permute-start.9 = (f32[128,128]{1,0:T(8,128)S(1)}, f32[128,128]{1,0:T(8,128)S(1)}, u32[]{:S(2)}, u32[]{:S(2)}) collective-permute-start(f32[128,128]{1,0:T(8,128)S(1)} %get-tuple-element.14), channel_id=1, source_target_pairs={{0,64},{16,80},{32,96},{48,112},{64,0},{80,16},{96,32},{112,48},{1... | collective-permute-start | bytes 196616 | tf_op jit(solution)/shard_map/ppermute | solution.py:296
  87.7 23.9 %collective-permute-start.8 = (f32[128,128]{1,0:T(8,128)S(1)}, f32[128,128]{1,0:T(8,128)S(1)}, u32[]{:S(2)}, u32[]{:S(2)}) collective-permute-start(f32[128,128]{1,0:T(8,128)S(1)} %get-tuple-element.14), channel_id=1, source_target_pairs={{0,32},{16,48},{32,0},{48,16},{64,96},{80,112},{96,64},{112,80},{1... | collective-permute-start | bytes 196616 | tf_op jit(solution)/shard_map/ppermute | solution.py:296
  111.6 4.3 %collective-permute-start.12 = (f32[128,128]{1,0:T(8,128)S(1)}, f32[128,128]{1,0:T(8,128)S(1)}, u32[]{:S(2)}, u32[]{:S(2)}) collective-permute-start(f32[128,128]{1,0:T(8,128)S(1)} %collective-permute-done.10), channel_id=1, source_target_pairs={{0,64},{16,80},{32,96},{48,112},{64,0},{80,16},{96,32},{112,48},{1... | collective-permute-start | bytes 196616 | tf_op jit(solution)/shard_map/ppermute | solution.py:296
  114.0 4.4 %collective-permute-start.11 = (f32[2,128,128]{2,1,0:T(8,128)S(1)}, f32[2,128,128]{2,1,0:T(8,128)S(1)}, u32[]{:S(2)}, u32[]{:S(2)}) collective-permute-start(f32[2,128,128]{2,1,0:T(8,128)S(1)} %pad_maximum_fusion.3), channel_id=1, source_target_pairs={{0,32},{16,48},{32,0},{48,16},{64,96},{80,112},{96,64},{112,80},{1... | collective-permute-start | bytes 393224 | tf_op jit(solution)/shard_map/ppermute | solution.py:296
  114.8 12.1 %copy-start.4 = (f32[8,128,128]{2,1,0:T(8,128)S(1)}, f32[8,128,128]{2,1,0:T(8,128)}, u32[]{:S(2)}) copy-start(f32[8,128,128]{2,1,0:T(8,128)} %alda_ref.1) | copy-start | bytes 1572868
  114.8 12.2 %copy-start.5 = (f32[8,128,128]{2,1,0:T(8,128)S(1)}, f32[8,128,128]{2,1,0:T(8,128)}, u32[]{:S(2)}) copy-start(f32[8,128,128]{2,1,0:T(8,128)} %local_ref.1) | copy-start | bytes 1572868
  114.8 5.9 %collective-permute-start.14 = (f32[4,128,128]{2,1,0:T(8,128)S(1)}, f32[4,128,128]{2,1,0:T(8,128)S(1)}, u32[]{:S(2)}, u32[]{:S(2)}) collective-permute-start(f32[4,128,128]{2,1,0:T(8,128)S(1)} %pad_maximum_fusion.1), channel_id=1, source_target_pairs={{0,16},{16,0},{32,48},{48,32},{64,80},{80,64},{96,112},{112,96},{1... | collective-permute-start | bytes 786440 | tf_op jit(solution)/shard_map/ppermute | solution.py:296
  118.5 8.3 %collective-permute-start.15 = (f32[4,128,128]{2,1,0:T(8,128)S(1)}, f32[4,128,128]{2,1,0:T(8,128)S(1)}, u32[]{:S(2)}, u32[]{:S(2)}) collective-permute-start(f32[4,128,128]{2,1,0:T(8,128)S(1)} %pad_maximum_fusion.2), channel_id=1, source_target_pairs={{0,16},{16,0},{32,48},{48,32},{64,80},{80,64},{96,112},{112,96},{1... | collective-permute-start | bytes 786440 | tf_op jit(solution)/shard_map/ppermute | solution.py:296
  131.8 33.6 %copy-start.6 = (bf16[2,256,256]{2,1,0:T(8,128)(2,1)S(1)}, bf16[2,256,256]{2,1,0:T(8,128)(2,1)}, u32[]{:S(2)}) copy-start(bf16[2,256,256]{2,1,0:T(8,128)(2,1)} %constant.62.clone.x_ref) | copy-start | bytes 786436
  (2 other events, 24.3 us)
where the time goes:
time: 168 us
  starting transfers between devices  56.1 us (33%)
  waiting for transfers between devices  51.2 us (30%)
  blocking collectives  43.8 us (26%)
  Pallas kernels  13.6 us (8%)
    all_to_all x2, blocking collectives, exchange(): return lax.all_to_all(array, axis, split_axis=0, concat_axis=0, tiled=True)  43.8 us
    ppermute x16, waiting for transfers between devices, partner(): lax.ppermute(array, 'band', [(i, i ^ mask) for i in range(lax.axis_size('...  43.8 us
    all_to_all x3, starting transfers between devices, exchange(): return lax.all_to_all(array, axis, split_axis=0, concat_axis=0, tiled=True)  28.4 us
    ppermute x16, starting transfers between devices, partner(): lax.ppermute(array, 'band', [(i, i ^ mask) for i in range(lax.axis_size('...  27.7 us
    all_to_all x3, waiting for transfers between devices, exchange(): return lax.all_to_all(array, axis, split_axis=0, concat_axis=0, tiled=True)  7.48 us
    pallas_call x1, Pallas kernels, per_device(): call(density_kernel, [some, some, (parts, 2, half, share, length)], grant...  4.17 us
    pallas_call x1, Pallas kernels, per_device(): call(field_kernel, (parts, 2, 2, share, share, length), grid=steps, in_sp...  3.78 us
  transfers between devices with their start and end apart: 19, of which 9 were waited for; matrix products, arithmetic and copies ran while one was open for 1% of the time, Pallas kernels for 1%

commit v1 on v0

--- a/solution.py
+++ b/solution.py
@@ -129,7 +129,8 @@
                     continue
                 for n in range(parts):
                     tile = block[n * share : (n + 1) * share]
-                    mixed_ref[(n ^ me) & 1, (n ^ me) >> 1, part, x] = tile
+                    steps = ((n >> 1) - (me >> 1)) & (parts // 2 - 1)
+                    mixed_ref[(n ^ me) & 1, steps, part, x] = tile
         for copy in outs[i]:
             copy.start()
     for copy in outs[0] + outs[1]:
@@ -296,6 +297,11 @@
     return lax.ppermute(array, "band", [(i, i ^ mask) for i in range(lax.axis_size("band"))])
 
 
+def ahead(array, steps):
+    count = lax.axis_size("band")
+    return lax.ppermute(array, "band", [(i, (i + steps) % count) for i in range(count)])
+
+
 def per_device(orbitals, trials, alda_kernel, local_potential, band_energies):
     length = orbitals.shape[2]
     parts = lax.axis_size("band")
@@ -341,7 +347,7 @@
     )(me.reshape(1), orbitals, trials, tables["up"], tables["down"])
     near = partner(near.reshape(parts // 2, points, length), 1)
     near = near + kept.reshape(parts // 2, points, length)
-    near = [near[0]] + [partner(near[i], 2 * i) for i in range(1, parts // 2)]
+    near = [near[0]] + [ahead(near[i], 2 * i) for i in range(1, parts // 2)]
     pieces = exchange(pieces.reshape(parts, points, length), "band")
     spectrum, lines = call(
         share_kernel, [(2 * points, length), (parts, 2 * share, length)]

time: 168 us -> 168 us (level)
    ppermute x0 -> x7, starting transfers between devices: none -> 16.3 us  [ahead(): lax.ppermute(array, 'band', [(i, (i + steps) % count) for i in range(coun...]
    ppermute x16 -> x9, starting transfers between devices: 27.7 us -> 13.4 us  [partner(): lax.ppermute(array, 'band', [(i, i ^ mask) for i in range(lax.axis_size('...]
    ppermute x16 -> x9, waiting for transfers between devices: 43.8 us -> 40.5 us  [partner(): lax.ppermute(array, 'band', [(i, i ^ mask) for i in range(lax.axis_size('...]
    ppermute x0 -> x7, waiting for transfers between devices: none -> 3.07 us  [ahead(): lax.ppermute(array, 'band', [(i, (i + steps) % count) for i in range(coun...]
    all_to_all x3, starting transfers between devices: 28.4 us -> 26.6 us  [exchange(): return lax.all_to_all(array, axis, split_axis=0, concat_axis=0, tiled=True)]
where the time goes in v1:
time: 168 us
  starting transfers between devices  56.4 us (34%)
  waiting for transfers between devices  51 us (30%)
  blocking collectives  43.9 us (26%)
  Pallas kernels  13.6 us (8%)
    all_to_all x2, blocking collectives, exchange(): return lax.all_to_all(array, axis, split_axis=0, concat_axis=0, tiled=True)  43.9 us
    ppermute x9, waiting for transfers between devices, partner(): lax.ppermute(array, 'band', [(i, i ^ mask) for i in range(lax.axis_size('...  40.5 us
    all_to_all x3, starting transfers between devices, exchange(): return lax.all_to_all(array, axis, split_axis=0, concat_axis=0, tiled=True)  26.6 us
    ppermute x7, starting transfers between devices, ahead(): lax.ppermute(array, 'band', [(i, (i + steps) % count) for i in range(coun...  16.3 us
    ppermute x9, starting transfers between devices, partner(): lax.ppermute(array, 'band', [(i, i ^ mask) for i in range(lax.axis_size('...  13.4 us
    all_to_all x3, waiting for transfers between devices, exchange(): return lax.all_to_all(array, axis, split_axis=0, concat_axis=0, tiled=True)  7.48 us
    pallas_call x1, Pallas kernels, per_device(): call(density_kernel, [some, some, (parts, 2, half, share, length)], grant...  4.17 us
    pallas_call x1, Pallas kernels, per_device(): call(field_kernel, (parts, 2, 2, share, share, length), grid=steps, in_sp...  3.78 us
  transfers between devices with their start and end apart: 19, of which 9 were waited for; matrix products, arithmetic and copies ran while one was open for 1% of the time, Pallas kernels for 1%

profile of v1, /device:TPU:1, one launch (start us, length us, event | category | flops | bytes accessed | tf_op | source)
XLA Modules:
  0.0 167.9 jit_solution(11494488643014985831)
XLA Ops:
  0.6 4.2 %shard_map.95 = (f32[8,2,4,8,128]{4,3,2,1,0:T(8,128)}, f32[8,2,4,8,128]{4,3,2,1,0:T(8,128)}, f32[16,2,4,8,128]{4,3,2,1,0:T(8,128)}) custom-call(s32[1]{0:T(128)} %bitcast.me_ref, bf16[1,8,128,128]{3,2,1,0:T(8,128)(2,1)} %orbital_ref.3, bf16[2,1,8,128,128]{4,3,2,1,0:T(8,128)(2,1)} %trial_ref.1, bf16[2,256,256]{2,1,0:T(8,128)(2,1)} %constant.61.clone.up_in.up_ref, ...), custom_call_target="tpu_custom_call" | custom-call | tf_op jit(solution)/shard_map/pallas_call | solution.py:330
  4.8 10.3 %all-to-all-start = ((f32[16,64,128]{2,1,0:T(8,128)}), f32[16,64,128]{2,1,0:T(8,128)S(1)}, u32[]{:S(2)}, u32[]{:S(2)}) async-start(f32[16,64,128]{2,1,0:T(8,128)} %bitcast.51), calls=%async_computation | async-start | bytes 1048576 | tf_op jit(solution)/shard_map/all_to_all | solution.py:293
  15.1 1.4 collective-permute-start
  16.5 6.7 %collective-permute-done = f32[8,64,128]{2,1,0:T(8,128)S(1)} collective-permute-done((f32[8,64,128]{2,1,0:T(8,128)}, f32[8,64,128]{2,1,0:T(8,128)S(1)}, u32[]{:S(2)}, u32[]{:S(2)}) %collective-permute-start) | collective-permute-done | bytes 262176 | tf_op jit(solution)/shard_map/ppermute | solution.py:297
  24.2 3.5 %collective-permute-start.7 = (f32[64,128]{1,0:T(8,128)S(1)}, f32[64,128]{1,0:T(8,128)S(1)}, u32[]{:S(2)}, u32[]{:S(2)}) collective-permute-start(f32[64,128]{1,0:T(8,128)S(1)} %get-tuple-element.18), channel_id=1, source_target_pairs={{0,224},{16,240},{32,0},{48,16},{64,32},{80,48},{96,64},{112,80},{... | collective-permute-start | bytes 98312 | tf_op jit(solution)/shard_map/ppermute | solution.py:302
  27.7 1.7 %collective-permute-start.6 = (f32[64,128]{1,0:T(8,128)S(1)}, f32[64,128]{1,0:T(8,128)S(1)}, u32[]{:S(2)}, u32[]{:S(2)}) collective-permute-start(f32[64,128]{1,0:T(8,128)S(1)} %get-tuple-element.19), channel_id=1, source_target_pairs={{0,192},{16,208},{32,224},{48,240},{64,0},{80,16},{96,32},{112,48}... | collective-permute-start | bytes 98312 | tf_op jit(solution)/shard_map/ppermute | solution.py:302
  29.4 3.2 %collective-permute-start.5 = (f32[64,128]{1,0:T(8,128)S(1)}, f32[64,128]{1,0:T(8,128)S(1)}, u32[]{:S(2)}, u32[]{:S(2)}) collective-permute-start(f32[64,128]{1,0:T(8,128)S(1)} %get-tuple-element.20), channel_id=1, source_target_pairs={{0,160},{16,176},{32,192},{48,208},{64,224},{80,240},{96,0},{112,1... | collective-permute-start | bytes 98312 | tf_op jit(solution)/shard_map/ppermute | solution.py:302
  33.4 2.5 %collective-permute-start.3 = (f32[64,128]{1,0:T(8,128)S(1)}, f32[64,128]{1,0:T(8,128)S(1)}, u32[]{:S(2)}, u32[]{:S(2)}) collective-permute-start(f32[64,128]{1,0:T(8,128)S(1)} %get-tuple-element.22), channel_id=1, source_target_pairs={{0,96},{16,112},{32,128},{48,144},{64,160},{80,176},{96,192},{112,... | collective-permute-start | bytes 98312 | tf_op jit(solution)/shard_map/ppermute | solution.py:302
  35.9 3.3 %collective-permute-start.2 = (f32[64,128]{1,0:T(8,128)S(1)}, f32[64,128]{1,0:T(8,128)S(1)}, u32[]{:S(2)}, u32[]{:S(2)}) collective-permute-start(f32[64,128]{1,0:T(8,128)S(1)} %get-tuple-element.23), channel_id=1, source_target_pairs={{0,64},{16,80},{32,96},{48,112},{64,128},{80,144},{96,160},{112,17... | collective-permute-start | bytes 98312 | tf_op jit(solution)/shard_map/ppermute | solution.py:302
  39.2 1.4 collective-permute-start.1
  41.6 2.1 %collective-permute-done.1.refs_1_ = f32[64,128]{1,0:T(8,128)S(1)} collective-permute-done((f32[64,128]{1,0:T(8,128)S(1)}, f32[64,128]{1,0:T(8,128)S(1)}, u32[]{:S(2)}, u32[]{:S(2)}) %collective-permute-start.1) | collective-permute-done | bytes 32800 | tf_op jit(solution)/shard_map/ppermute | solution.py:302
  44.4 11.8 %all-to-all-start.1 = ((f32[16,16,128]{2,1,0:T(8,128)}), f32[16,16,128]{2,1,0:T(8,128)S(1)}, u32[]{:S(2)}, u32[]{:S(2)}) async-start(f32[16,16,128]{2,1,0:T(8,128)} %get-tuple-element.13), calls=%async_computation.1 | async-start | bytes 262144 | tf_op jit(solution)/shard_map/all_to_all | solution.py:293
  56.3 7.5 %all-to-all-done.1.pieces_ref = f32[16,16,128]{2,1,0:T(8,128)S(1)} async-done(((f32[16,16,128]{2,1,0:T(8,128)}), f32[16,16,128]{2,1,0:T(8,128)S(1)}, u32[]{:S(2)}, u32[]{:S(2)}) %all-to-all-start.1) | async-done | bytes 131104 | tf_op jit(solution)/shard_map/all_to_all | solution.py:293
  64.3 10.3 %all_to_all.25 = f32[16,8,128]{2,1,0:T(8,128)S(1)} all-to-all(f32[16,8,128]{2,1,0:T(8,128)S(1)} %shard_map.97), channel_id=1, replica_groups=mesh['band'=16,'grid'=16] {'grid'}, dimensions={0} | all-to-all | bytes 131072 | tf_op jit(solution)/shard_map/all_to_all | solution.py:293
  75.6 4.5 %all-to-all-start.3 = ((f32[16,128,128]{2,1,0:T(8,128)}), f32[16,128,128]{2,1,0:T(8,128)S(1)}, u32[]{:S(2)}, u32[]{:S(2)}) async-start(f32[16,128,128]{2,1,0:T(8,128)} %shard_map.98), calls=%async_computation.3 | async-start | bytes 2097152 | tf_op jit(solution)/shard_map/all_to_all | solution.py:293
  80.8 2.7 %collective-permute-start.13 = (f32[128,128]{1,0:T(8,128)S(1)}, f32[128,128]{1,0:T(8,128)S(1)}, u32[]{:S(2)}, u32[]{:S(2)}) collective-permute-start(f32[128,128]{1,0:T(8,128)S(1)} %get-tuple-element.14), channel_id=1, source_target_pairs={{0,224},{16,240},{32,192},{48,208},{64,160},{80,176},{96,128},{112... | collective-permute-start | bytes 196616 | tf_op jit(solution)/shard_map/ppermute | solution.py:297
  83.5 3.0 %collective-permute-start.10 = (f32[128,128]{1,0:T(8,128)S(1)}, f32[128,128]{1,0:T(8,128)S(1)}, u32[]{:S(2)}, u32[]{:S(2)}) collective-permute-start(f32[128,128]{1,0:T(8,128)S(1)} %get-tuple-element.14), channel_id=1, source_target_pairs={{0,128},{16,144},{32,160},{48,176},{64,192},{80,208},{96,224},{112... | collective-permute-start | bytes 196616 | tf_op jit(solution)/shard_map/ppermute | solution.py:297
  87.7 22.7 %collective-permute-done.10 = f32[128,128]{1,0:T(8,128)S(1)} collective-permute-done((f32[128,128]{1,0:T(8,128)S(1)}, f32[128,128]{1,0:T(8,128)S(1)}, u32[]{:S(2)}, u32[]{:S(2)}) %collective-permute-start.10) | collective-permute-done | bytes 65568 | tf_op jit(solution)/shard_map/ppermute | solution.py:297
  111.5 2.5 %collective-permute-start.12 = (f32[128,128]{1,0:T(8,128)S(1)}, f32[128,128]{1,0:T(8,128)S(1)}, u32[]{:S(2)}, u32[]{:S(2)}) collective-permute-start(f32[128,128]{1,0:T(8,128)S(1)} %collective-permute-done.10), channel_id=1, source_target_pairs={{0,64},{16,80},{32,96},{48,112},{64,0},{80,16},{96,32},{112,48},{1... | collective-permute-start | bytes 196616 | tf_op jit(solution)/shard_map/ppermute | solution.py:297
  115.9 2.5 %collective-permute-done.11 = f32[2,128,128]{2,1,0:T(8,128)S(1)} collective-permute-done((f32[2,128,128]{2,1,0:T(8,128)S(1)}, f32[2,128,128]{2,1,0:T(8,128)S(1)}, u32[]{:S(2)}, u32[]{:S(2)}) %collective-permute-start.11) | collective-permute-done | bytes 131104 | tf_op jit(solution)/shard_map/ppermute | solution.py:297
  120.8 6.0 %collective-permute-done.15 = f32[4,128,128]{2,1,0:T(8,128)S(1)} collective-permute-done((f32[4,128,128]{2,1,0:T(8,128)S(1)}, f32[4,128,128]{2,1,0:T(8,128)S(1)}, u32[]{:S(2)}, u32[]{:S(2)}) %collective-permute-start.15) | collective-permute-done | bytes 262176 | tf_op jit(solution)/shard_map/ppermute | solution.py:297
  128.0 3.8 %shard_map.100 = f32[16,2,2,8,8,128]{5,4,3,2,1,0:T(8,128)S(1)} custom-call(f32[16,2,8,8,128]{4,3,2,1,0:T(8,128)S(1)} %bitcast.40, bf16[1,8,128,128]{3,2,1,0:T(8,128)(2,1)S(1)} %copy-done.2, f32[2,8,128,128]{3,2,1,0:T(8,128)S(1)} %shard_map.99.base_ref, bf16[2,256,256]{2,1,0:T(8,128)(2,1)S(1)} %copy-done.1, bf16[2,256,256]{2,1,0:T(8,128)(2,1)S(1)} %copy-done), custom_call_target="tpu_custom_call" | custom-call | tf_op jit(solution)/shard_map/pallas_call | solution.py:398
  131.8 33.7 %all_to_all.26.pieces_ref = f32[16,256,128]{2,1,0:T(8,128)S(1)} all-to-all(f32[16,256,128]{2,1,0:T(8,128)S(1)} %bitcast.39), channel_id=1, replica_groups=mesh['band'=16,'grid'=16] {'grid'}, dimensions={0} | all-to-all | bytes 4194304 | tf_op jit(solution)/shard_map/all_to_all | solution.py:293
  165.5 2.4 %shard_map.101 = (f32[2,1,8,128,128]{4,3,2,1,0:T(8,128)}, f32[2,1,8,128,128]{4,3,2,1,0:T(8,128)}) custom-call(f32[16,256,128]{2,1,0:T(8,128)S(1)} %all_to_all.26.pieces_ref, bf16[2,256,256]{2,1,0:T(8,128)(2,1)S(1)} %copy-done.6), custom_call_target="tpu_custom_call" | custom-call | tf_op jit(solution)/shard_map/pallas_call | solution.py:409
  (60 shorter events, 12.9 us)
Async XLA Ops:
  4.8 51.5 %copy-start.1 = (bf16[2,256,256]{2,1,0:T(8,128)(2,1)S(1)}, bf16[2,256,256]{2,1,0:T(8,128)(2,1)}, u32[]{:S(2)}) copy-start(bf16[2,256,256]{2,1,0:T(8,128)(2,1)} %constant.61.clone.up_in.up_ref) | copy-start | bytes 786436
  4.8 59.0 %copy-start = (bf16[2,256,256]{2,1,0:T(8,128)(2,1)S(1)}, bf16[2,256,256]{2,1,0:T(8,128)(2,1)}, u32[]{:S(2)}) copy-start(bf16[2,256,256]{2,1,0:T(8,128)(2,1)} %constant.60.clone.down_in.down_ref) | copy-start | bytes 786436
  4.8 38.8 %all-to-all-start = ((f32[16,64,128]{2,1,0:T(8,128)}), f32[16,64,128]{2,1,0:T(8,128)S(1)}, u32[]{:S(2)}, u32[]{:S(2)}) async-start(f32[16,64,128]{2,1,0:T(8,128)} %bitcast.51), calls=%async_computation | async-start | bytes 1048576 | tf_op jit(solution)/shard_map/all_to_all | solution.py:293
  15.1 8.1 %collective-permute-start = (f32[8,64,128]{2,1,0:T(8,128)}, f32[8,64,128]{2,1,0:T(8,128)S(1)}, u32[]{:S(2)}, u32[]{:S(2)}) collective-permute-start(f32[8,64,128]{2,1,0:T(8,128)} %bitcast.60), channel_id=1, source_target_pairs={{0,16},{16,0},{32,48},{48,32},{64,80},{80,64},{96,112},{112,96},{1... | collective-permute-start | bytes 786440 | tf_op jit(solution)/shard_map/ppermute | solution.py:297
  24.2 11.7 %collective-permute-start.7 = (f32[64,128]{1,0:T(8,128)S(1)}, f32[64,128]{1,0:T(8,128)S(1)}, u32[]{:S(2)}, u32[]{:S(2)}) collective-permute-start(f32[64,128]{1,0:T(8,128)S(1)} %get-tuple-element.18), channel_id=1, source_target_pairs={{0,224},{16,240},{32,0},{48,16},{64,32},{80,48},{96,64},{112,80},{... | collective-permute-start | bytes 98312 | tf_op jit(solution)/shard_map/ppermute | solution.py:302
  27.7 11.5 %collective-permute-start.6 = (f32[64,128]{1,0:T(8,128)S(1)}, f32[64,128]{1,0:T(8,128)S(1)}, u32[]{:S(2)}, u32[]{:S(2)}) collective-permute-start(f32[64,128]{1,0:T(8,128)S(1)} %get-tuple-element.19), channel_id=1, source_target_pairs={{0,192},{16,208},{32,224},{48,240},{64,0},{80,16},{96,32},{112,48}... | collective-permute-start | bytes 98312 | tf_op jit(solution)/shard_map/ppermute | solution.py:302
  29.4 11.2 %collective-permute-start.5 = (f32[64,128]{1,0:T(8,128)S(1)}, f32[64,128]{1,0:T(8,128)S(1)}, u32[]{:S(2)}, u32[]{:S(2)}) collective-permute-start(f32[64,128]{1,0:T(8,128)S(1)} %get-tuple-element.20), channel_id=1, source_target_pairs={{0,160},{16,176},{32,192},{48,208},{64,224},{80,240},{96,0},{112,1... | collective-permute-start | bytes 98312 | tf_op jit(solution)/shard_map/ppermute | solution.py:302
  32.6 8.0 %collective-permute-start.4 = (f32[64,128]{1,0:T(8,128)S(1)}, f32[64,128]{1,0:T(8,128)S(1)}, u32[]{:S(2)}, u32[]{:S(2)}) collective-permute-start(f32[64,128]{1,0:T(8,128)S(1)} %get-tuple-element.21), channel_id=1, source_target_pairs={{0,128},{16,144},{32,160},{48,176},{64,192},{80,208},{96,224},{112... | collective-permute-start | bytes 98312 | tf_op jit(solution)/shard_map/ppermute | solution.py:302
  33.4 7.2 %collective-permute-start.3 = (f32[64,128]{1,0:T(8,128)S(1)}, f32[64,128]{1,0:T(8,128)S(1)}, u32[]{:S(2)}, u32[]{:S(2)}) collective-permute-start(f32[64,128]{1,0:T(8,128)S(1)} %get-tuple-element.22), channel_id=1, source_target_pairs={{0,96},{16,112},{32,128},{48,144},{64,160},{80,176},{96,192},{112,... | collective-permute-start | bytes 98312 | tf_op jit(solution)/shard_map/ppermute | solution.py:302
  35.9 5.7 %collective-permute-start.2 = (f32[64,128]{1,0:T(8,128)S(1)}, f32[64,128]{1,0:T(8,128)S(1)}, u32[]{:S(2)}, u32[]{:S(2)}) collective-permute-start(f32[64,128]{1,0:T(8,128)S(1)} %get-tuple-element.23), channel_id=1, source_target_pairs={{0,64},{16,80},{32,96},{48,112},{64,128},{80,144},{96,160},{112,17... | collective-permute-start | bytes 98312 | tf_op jit(solution)/shard_map/ppermute | solution.py:302
  39.2 4.5 %collective-permute-start.1 = (f32[64,128]{1,0:T(8,128)S(1)}, f32[64,128]{1,0:T(8,128)S(1)}, u32[]{:S(2)}, u32[]{:S(2)}) collective-permute-start(f32[64,128]{1,0:T(8,128)S(1)} %get-tuple-element.24), channel_id=1, source_target_pairs={{0,32},{16,48},{32,64},{48,80},{64,96},{80,112},{96,128},{112,144}... | collective-permute-start | bytes 98312 | tf_op jit(solution)/shard_map/ppermute | solution.py:302
  44.4 19.4 %all-to-all-start.1 = ((f32[16,16,128]{2,1,0:T(8,128)}), f32[16,16,128]{2,1,0:T(8,128)S(1)}, u32[]{:S(2)}, u32[]{:S(2)}) async-start(f32[16,16,128]{2,1,0:T(8,128)} %get-tuple-element.13), calls=%async_computation.1 | async-start | bytes 262144 | tf_op jit(solution)/shard_map/all_to_all | solution.py:293
  75.6 52.4 %all-to-all-start.3 = ((f32[16,128,128]{2,1,0:T(8,128)}), f32[16,128,128]{2,1,0:T(8,128)S(1)}, u32[]{:S(2)}, u32[]{:S(2)}) async-start(f32[16,128,128]{2,1,0:T(8,128)} %shard_map.98), calls=%async_computation.3 | async-start | bytes 2097152 | tf_op jit(solution)/shard_map/all_to_all | solution.py:293
  80.8 35.0 %collective-permute-start.13 = (f32[128,128]{1,0:T(8,128)S(1)}, f32[128,128]{1,0:T(8,128)S(1)}, u32[]{:S(2)}, u32[]{:S(2)}) collective-permute-start(f32[128,128]{1,0:T(8,128)S(1)} %get-tuple-element.14), channel_id=1, source_target_pairs={{0,224},{16,240},{32,192},{48,208},{64,160},{80,176},{96,128},{112... | collective-permute-start | bytes 196616 | tf_op jit(solution)/shard_map/ppermute | solution.py:297
  83.5 26.8 %collective-permute-start.10 = (f32[128,128]{1,0:T(8,128)S(1)}, f32[128,128]{1,0:T(8,128)S(1)}, u32[]{:S(2)}, u32[]{:S(2)}) collective-permute-start(f32[128,128]{1,0:T(8,128)S(1)} %get-tuple-element.14), channel_id=1, source_target_pairs={{0,128},{16,144},{32,160},{48,176},{64,192},{80,208},{96,224},{112... | collective-permute-start | bytes 196616 | tf_op jit(solution)/shard_map/ppermute | solution.py:297
  86.5 23.8 %collective-permute-start.9 = (f32[128,128]{1,0:T(8,128)S(1)}, f32[128,128]{1,0:T(8,128)S(1)}, u32[]{:S(2)}, u32[]{:S(2)}) collective-permute-start(f32[128,128]{1,0:T(8,128)S(1)} %get-tuple-element.14), channel_id=1, source_target_pairs={{0,64},{16,80},{32,96},{48,112},{64,0},{80,16},{96,32},{112,48},{1... | collective-permute-start | bytes 196616 | tf_op jit(solution)/shard_map/ppermute | solution.py:297
  87.7 23.9 %collective-permute-start.8 = (f32[128,128]{1,0:T(8,128)S(1)}, f32[128,128]{1,0:T(8,128)S(1)}, u32[]{:S(2)}, u32[]{:S(2)}) collective-permute-start(f32[128,128]{1,0:T(8,128)S(1)} %get-tuple-element.14), channel_id=1, source_target_pairs={{0,32},{16,48},{32,0},{48,16},{64,96},{80,112},{96,64},{112,80},{1... | collective-permute-start | bytes 196616 | tf_op jit(solution)/shard_map/ppermute | solution.py:297
  111.5 4.4 %collective-permute-start.12 = (f32[128,128]{1,0:T(8,128)S(1)}, f32[128,128]{1,0:T(8,128)S(1)}, u32[]{:S(2)}, u32[]{:S(2)}) collective-permute-start(f32[128,128]{1,0:T(8,128)S(1)} %collective-permute-done.10), channel_id=1, source_target_pairs={{0,64},{16,80},{32,96},{48,112},{64,0},{80,16},{96,32},{112,48},{1... | collective-permute-start | bytes 196616 | tf_op jit(solution)/shard_map/ppermute | solution.py:297
  114.0 4.4 %collective-permute-start.11 = (f32[2,128,128]{2,1,0:T(8,128)S(1)}, f32[2,128,128]{2,1,0:T(8,128)S(1)}, u32[]{:S(2)}, u32[]{:S(2)}) collective-permute-start(f32[2,128,128]{2,1,0:T(8,128)S(1)} %pad_maximum_fusion.3), channel_id=1, source_target_pairs={{0,32},{16,48},{32,0},{48,16},{64,96},{80,112},{96,64},{112,80},{1... | collective-permute-start | bytes 393224 | tf_op jit(solution)/shard_map/ppermute | solution.py:297
  114.7 12.2 %copy-start.4 = (f32[8,128,128]{2,1,0:T(8,128)S(1)}, f32[8,128,128]{2,1,0:T(8,128)}, u32[]{:S(2)}) copy-start(f32[8,128,128]{2,1,0:T(8,128)} %alda_ref.1) | copy-start | bytes 1572868
  114.7 12.2 %copy-start.5 = (f32[8,128,128]{2,1,0:T(8,128)S(1)}, f32[8,128,128]{2,1,0:T(8,128)}, u32[]{:S(2)}) copy-start(f32[8,128,128]{2,1,0:T(8,128)} %local_ref.1) | copy-start | bytes 1572868
  114.8 6.0 %collective-permute-start.14 = (f32[4,128,128]{2,1,0:T(8,128)S(1)}, f32[4,128,128]{2,1,0:T(8,128)S(1)}, u32[]{:S(2)}, u32[]{:S(2)}) collective-permute-start(f32[4,128,128]{2,1,0:T(8,128)S(1)} %pad_maximum_fusion.1), channel_id=1, source_target_pairs={{0,16},{16,0},{32,48},{48,32},{64,80},{80,64},{96,112},{112,96},{1... | collective-permute-start | bytes 786440 | tf_op jit(solution)/shard_map/ppermute | solution.py:297
  118.5 8.4 %collective-permute-start.15 = (f32[4,128,128]{2,1,0:T(8,128)S(1)}, f32[4,128,128]{2,1,0:T(8,128)S(1)}, u32[]{:S(2)}, u32[]{:S(2)}) collective-permute-start(f32[4,128,128]{2,1,0:T(8,128)S(1)} %pad_maximum_fusion.2), channel_id=1, source_target_pairs={{0,16},{16,0},{32,48},{48,32},{64,80},{80,64},{96,112},{112,96},{1... | collective-permute-start | bytes 786440 | tf_op jit(solution)/shard_map/ppermute | solution.py:297
  131.8 33.7 %copy-start.6 = (bf16[2,256,256]{2,1,0:T(8,128)(2,1)S(1)}, bf16[2,256,256]{2,1,0:T(8,128)(2,1)}, u32[]{:S(2)}) copy-start(bf16[2,256,256]{2,1,0:T(8,128)(2,1)} %constant.62.clone.x_ref) | copy-start | bytes 786436
  (2 other events, 24.4 us)

commit v2 on v0

--- a/solution.py
+++ b/solution.py
@@ -247,10 +247,12 @@
                 out_ref[:, k, part, x] = block.reshape(parts, length // parts, length)
 
 
-def final_kernel(pieces_ref, x_ref, real_ref, imag_ref):
+def final_kernel(pieces_ref, x_ref, real_hbm, imag_hbm, real_ref, imag_ref, sems):
     length = real_ref.shape[-1]
     share = real_ref.shape[2]
     table = pair(x_ref)
+    group = share // 2
+    copies = []
     for k in range(2):
         for b in range(share):
             parts = []
@@ -261,6 +263,16 @@
             turned = product(split(jnp.concatenate(parts, axis=0).T), table)
             real_ref[k, 0, b] = turned[:, :length]
             imag_ref[k, 0, b] = turned[:, length:]
+            if (b + 1) % group == 0:
+                done = (k, 0, pl.ds(b + 1 - group, group))
+                for source, target in ((real_ref, real_hbm), (imag_ref, imag_hbm)):
+                    copy = pltpu.make_async_copy(
+                        source.at[done], target.at[done], sems.at[len(copies)]
+                    )
+                    copy.start()
+                    copies.append(copy)
+    for copy in copies:
+        copy.wait()
 
 
 def signed(positions, length):
@@ -400,7 +412,20 @@
     )(potential, orbitals, base, tables["up"], tables["down"])
     received = exchange(fields.reshape(parts, 4 * points, length), "grid")
     shape = (2, 1, share, length, length)
-    return tuple(call(final_kernel, [shape, shape])(received, tables["last"]))
+    vector = pl.BlockSpec(memory_space=pltpu.VMEM)
+    return tuple(
+        call(
+            final_kernel,
+            [shape, shape],
+            in_specs=[vector] * 2,
+            out_specs=[pl.BlockSpec(memory_space=pltpu.HBM)] * 2,
+            scratch_shapes=[
+                pltpu.VMEM(shape, WIDE),
+                pltpu.VMEM(shape, WIDE),
+                pltpu.SemaphoreType.DMA((8,)),
+            ],
+        )(received, tables["last"])
+    )
 
 
 def solution(mesh):

time: 168 us -> 168 us (level)
  no operation moved by 1% of the time
where the time goes in v2:
time: 168 us; the launch traced here: 167 us
  starting transfers between devices  56.1 us (33%)
  waiting for transfers between devices  51.2 us (30%)
  blocking collectives  43.8 us (26%)
  Pallas kernels  13.2 us (8%)
  between operations  1.71 us (1%)
    all_to_all x2, blocking collectives, exchange(): return lax.all_to_all(array, axis, split_axis=0, concat_axis=0, tiled=True)  43.8 us
    ppermute x16, waiting for transfers between devices, partner(): lax.ppermute(array, 'band', [(i, i ^ mask) for i in range(lax.axis_size('...  43.8 us
    all_to_all x3, starting transfers between devices, exchange(): return lax.all_to_all(array, axis, split_axis=0, concat_axis=0, tiled=True)  28.4 us
    ppermute x16, starting transfers between devices, partner(): lax.ppermute(array, 'band', [(i, i ^ mask) for i in range(lax.axis_size('...  27.7 us
    all_to_all x3, waiting for transfers between devices, exchange(): return lax.all_to_all(array, axis, split_axis=0, concat_axis=0, tiled=True)  7.48 us
    pallas_call x1, Pallas kernels, per_device(): call(density_kernel, [some, some, (parts, 2, half, share, length)], grant...  4.17 us
    pallas_call x1, Pallas kernels, per_device(): call(field_kernel, (parts, 2, 2, share, share, length), grid=steps, in_sp...  3.78 us
  transfers between devices with their start and end apart: 19, of which 9 were waited for; matrix products, arithmetic and copies ran while one was open for 1% of the time, Pallas kernels for 1%

profile of v2, /device:TPU:1, one launch (start us, length us, event | category | flops | bytes accessed | tf_op | source)
XLA Modules:
  0.0 167.5 jit_solution(3255215488935691827)
XLA Ops:
  0.6 4.2 %shard_map.95 = (f32[8,2,4,8,128]{4,3,2,1,0:T(8,128)}, f32[8,2,4,8,128]{4,3,2,1,0:T(8,128)}, f32[16,2,4,8,128]{4,3,2,1,0:T(8,128)}) custom-call(s32[1]{0:T(128)} %bitcast.me_ref, bf16[1,8,128,128]{3,2,1,0:T(8,128)(2,1)} %orbital_ref.3, bf16[2,1,8,128,128]{4,3,2,1,0:T(8,128)(2,1)} %trial_ref.1, bf16[2,256,256]{2,1,0:T(8,128)(2,1)} %constant.61.clone.up_in.up_ref, ...), custom_call_target="tpu_custom_call" | custom-call | tf_op jit(solution)/shard_map/pallas_call | solution.py:336
  4.8 10.3 %all-to-all-start = ((f32[16,64,128]{2,1,0:T(8,128)}), f32[16,64,128]{2,1,0:T(8,128)S(1)}, u32[]{:S(2)}, u32[]{:S(2)}) async-start(f32[16,64,128]{2,1,0:T(8,128)} %bitcast.51), calls=%async_computation | async-start | bytes 1048576 | tf_op jit(solution)/shard_map/all_to_all | solution.py:304
  15.1 1.4 collective-permute-start
  16.5 6.7 %collective-permute-done = f32[8,64,128]{2,1,0:T(8,128)S(1)} collective-permute-done((f32[8,64,128]{2,1,0:T(8,128)}, f32[8,64,128]{2,1,0:T(8,128)S(1)}, u32[]{:S(2)}, u32[]{:S(2)}) %collective-permute-start) | collective-permute-done | bytes 262176 | tf_op jit(solution)/shard_map/ppermute | solution.py:308
  24.2 3.5 %collective-permute-start.7 = (f32[64,128]{1,0:T(8,128)S(1)}, f32[64,128]{1,0:T(8,128)S(1)}, u32[]{:S(2)}, u32[]{:S(2)}) collective-permute-start(f32[64,128]{1,0:T(8,128)S(1)} %get-tuple-element.18), channel_id=1, source_target_pairs={{0,224},{16,240},{32,192},{48,208},{64,160},{80,176},{96,128},{112... | collective-permute-start | bytes 98312 | tf_op jit(solution)/shard_map/ppermute | solution.py:308
  27.7 1.8 %collective-permute-start.6 = (f32[64,128]{1,0:T(8,128)S(1)}, f32[64,128]{1,0:T(8,128)S(1)}, u32[]{:S(2)}, u32[]{:S(2)}) collective-permute-start(f32[64,128]{1,0:T(8,128)S(1)} %get-tuple-element.19), channel_id=1, source_target_pairs={{0,192},{16,208},{32,224},{48,240},{64,128},{80,144},{96,160},{112... | collective-permute-start | bytes 98312 | tf_op jit(solution)/shard_map/ppermute | solution.py:308
  29.5 5.4 %collective-permute-start.5 = (f32[64,128]{1,0:T(8,128)S(1)}, f32[64,128]{1,0:T(8,128)S(1)}, u32[]{:S(2)}, u32[]{:S(2)}) collective-permute-start(f32[64,128]{1,0:T(8,128)S(1)} %get-tuple-element.20), channel_id=1, source_target_pairs={{0,160},{16,176},{32,128},{48,144},{64,224},{80,240},{96,192},{112... | collective-permute-start | bytes 98312 | tf_op jit(solution)/shard_map/ppermute | solution.py:308
  34.9 3.1 %collective-permute-start.3 = (f32[64,128]{1,0:T(8,128)S(1)}, f32[64,128]{1,0:T(8,128)S(1)}, u32[]{:S(2)}, u32[]{:S(2)}) collective-permute-start(f32[64,128]{1,0:T(8,128)S(1)} %get-tuple-element.22), channel_id=1, source_target_pairs={{0,96},{16,112},{32,64},{48,80},{64,32},{80,48},{96,0},{112,16},{1... | collective-permute-start | bytes 98312 | tf_op jit(solution)/shard_map/ppermute | solution.py:308
  38.5 3.4 %collective-permute-done.4.refs_4_ = f32[64,128]{1,0:T(8,128)S(1)} collective-permute-done((f32[64,128]{1,0:T(8,128)S(1)}, f32[64,128]{1,0:T(8,128)S(1)}, u32[]{:S(2)}, u32[]{:S(2)}) %collective-permute-start.4) | collective-permute-done | bytes 32800 | tf_op jit(solution)/shard_map/ppermute | solution.py:308
  42.6 12.1 %all-to-all-start.1 = ((f32[16,16,128]{2,1,0:T(8,128)}), f32[16,16,128]{2,1,0:T(8,128)S(1)}, u32[]{:S(2)}, u32[]{:S(2)}) async-start(f32[16,16,128]{2,1,0:T(8,128)} %get-tuple-element.13), calls=%async_computation.1 | async-start | bytes 262144 | tf_op jit(solution)/shard_map/all_to_all | solution.py:304
  54.9 7.5 %all-to-all-done.1.pieces_ref = f32[16,16,128]{2,1,0:T(8,128)S(1)} async-done(((f32[16,16,128]{2,1,0:T(8,128)}), f32[16,16,128]{2,1,0:T(8,128)S(1)}, u32[]{:S(2)}, u32[]{:S(2)}) %all-to-all-start.1) | async-done | bytes 131104 | tf_op jit(solution)/shard_map/all_to_all | solution.py:304
  62.9 10.3 %all_to_all.25 = f32[16,8,128]{2,1,0:T(8,128)S(1)} all-to-all(f32[16,8,128]{2,1,0:T(8,128)S(1)} %shard_map.97), channel_id=1, replica_groups=mesh['band'=16,'grid'=16] {'grid'}, dimensions={0} | all-to-all | bytes 131072 | tf_op jit(solution)/shard_map/all_to_all | solution.py:304
  74.2 6.0 %all-to-all-start.3 = ((f32[16,128,128]{2,1,0:T(8,128)}), f32[16,128,128]{2,1,0:T(8,128)S(1)}, u32[]{:S(2)}, u32[]{:S(2)}) async-start(f32[16,128,128]{2,1,0:T(8,128)} %shard_map.98), calls=%async_computation.3 | async-start | bytes 2097152 | tf_op jit(solution)/shard_map/all_to_all | solution.py:304
  80.9 2.7 %collective-permute-start.13 = (f32[128,128]{1,0:T(8,128)S(1)}, f32[128,128]{1,0:T(8,128)S(1)}, u32[]{:S(2)}, u32[]{:S(2)}) collective-permute-start(f32[128,128]{1,0:T(8,128)S(1)} %get-tuple-element.14), channel_id=1, source_target_pairs={{0,224},{16,240},{32,192},{48,208},{64,160},{80,176},{96,128},{112... | collective-permute-start | bytes 196616 | tf_op jit(solution)/shard_map/ppermute | solution.py:308
  83.5 3.0 %collective-permute-start.10 = (f32[128,128]{1,0:T(8,128)S(1)}, f32[128,128]{1,0:T(8,128)S(1)}, u32[]{:S(2)}, u32[]{:S(2)}) collective-permute-start(f32[128,128]{1,0:T(8,128)S(1)} %get-tuple-element.14), channel_id=1, source_target_pairs={{0,128},{16,144},{32,160},{48,176},{64,192},{80,208},{96,224},{112... | collective-permute-start | bytes 196616 | tf_op jit(solution)/shard_map/ppermute | solution.py:308
  86.5 1.2 collective-permute-start.9
  87.7 22.7 %collective-permute-done.10 = f32[128,128]{1,0:T(8,128)S(1)} collective-permute-done((f32[128,128]{1,0:T(8,128)S(1)}, f32[128,128]{1,0:T(8,128)S(1)}, u32[]{:S(2)}, u32[]{:S(2)}) %collective-permute-start.10) | collective-permute-done | bytes 65568 | tf_op jit(solution)/shard_map/ppermute | solution.py:308
  110.4 1.2 collective-permute-done.8
  111.6 2.5 %collective-permute-start.12 = (f32[128,128]{1,0:T(8,128)S(1)}, f32[128,128]{1,0:T(8,128)S(1)}, u32[]{:S(2)}, u32[]{:S(2)}) collective-permute-start(f32[128,128]{1,0:T(8,128)S(1)} %collective-permute-done.10), channel_id=1, source_target_pairs={{0,64},{16,80},{32,96},{48,112},{64,0},{80,16},{96,32},{112,48},{1... | collective-permute-start | bytes 196616 | tf_op jit(solution)/shard_map/ppermute | solution.py:308
  115.9 2.6 %collective-permute-done.11 = f32[2,128,128]{2,1,0:T(8,128)S(1)} collective-permute-done((f32[2,128,128]{2,1,0:T(8,128)S(1)}, f32[2,128,128]{2,1,0:T(8,128)S(1)}, u32[]{:S(2)}, u32[]{:S(2)}) %collective-permute-start.11) | collective-permute-done | bytes 131104 | tf_op jit(solution)/shard_map/ppermute | solution.py:308
  120.7 6.1 %collective-permute-done.15 = f32[4,128,128]{2,1,0:T(8,128)S(1)} collective-permute-done((f32[4,128,128]{2,1,0:T(8,128)S(1)}, f32[4,128,128]{2,1,0:T(8,128)S(1)}, u32[]{:S(2)}, u32[]{:S(2)}) %collective-permute-start.15) | collective-permute-done | bytes 262176 | tf_op jit(solution)/shard_map/ppermute | solution.py:308
  128.0 3.8 %shard_map.100 = f32[16,2,2,8,8,128]{5,4,3,2,1,0:T(8,128)S(1)} custom-call(f32[16,2,8,8,128]{4,3,2,1,0:T(8,128)S(1)} %bitcast.40, bf16[1,8,128,128]{3,2,1,0:T(8,128)(2,1)S(1)} %copy-done.2, f32[2,8,128,128]{3,2,1,0:T(8,128)S(1)} %shard_map.99.base_ref, bf16[2,256,256]{2,1,0:T(8,128)(2,1)S(1)} %copy-done.1, bf16[2,256,256]{2,1,0:T(8,128)(2,1)S(1)} %copy-done), custom_call_target="tpu_custom_call" | custom-call | tf_op jit(solution)/shard_map/pallas_call | solution.py:404
  131.8 33.6 %all_to_all.26.pieces_ref = f32[16,256,128]{2,1,0:T(8,128)S(1)} all-to-all(f32[16,256,128]{2,1,0:T(8,128)S(1)} %bitcast.39), channel_id=1, replica_groups=mesh['band'=16,'grid'=16] {'grid'}, dimensions={0} | all-to-all | bytes 4194304 | tf_op jit(solution)/shard_map/all_to_all | solution.py:304
  165.4 1.9 %shard_map.101 = (f32[2,1,8,128,128]{4,3,2,1,0:T(8,128)}, f32[2,1,8,128,128]{4,3,2,1,0:T(8,128)}) custom-call(f32[16,256,128]{2,1,0:T(8,128)S(1)} %all_to_all.26.pieces_ref, bf16[2,256,256]{2,1,0:T(8,128)(2,1)S(1)} %copy-done.6), custom_call_target="tpu_custom_call" | custom-call | tf_op jit(solution)/shard_map/pallas_call | solution.py:417
  (60 shorter events, 9.1 us)
Async XLA Ops:
  4.8 50.1 %copy-start.1 = (bf16[2,256,256]{2,1,0:T(8,128)(2,1)S(1)}, bf16[2,256,256]{2,1,0:T(8,128)(2,1)}, u32[]{:S(2)}) copy-start(bf16[2,256,256]{2,1,0:T(8,128)(2,1)} %constant.61.clone.up_in.up_ref) | copy-start | bytes 786436
  4.8 57.6 %copy-start = (bf16[2,256,256]{2,1,0:T(8,128)(2,1)S(1)}, bf16[2,256,256]{2,1,0:T(8,128)(2,1)}, u32[]{:S(2)}) copy-start(bf16[2,256,256]{2,1,0:T(8,128)(2,1)} %constant.60.clone.down_in.down_ref) | copy-start | bytes 786436
  4.8 37.0 %all-to-all-start = ((f32[16,64,128]{2,1,0:T(8,128)}), f32[16,64,128]{2,1,0:T(8,128)S(1)}, u32[]{:S(2)}, u32[]{:S(2)}) async-start(f32[16,64,128]{2,1,0:T(8,128)} %bitcast.51), calls=%async_computation | async-start | bytes 1048576 | tf_op jit(solution)/shard_map/all_to_all | solution.py:304
  15.1 8.1 %collective-permute-start = (f32[8,64,128]{2,1,0:T(8,128)}, f32[8,64,128]{2,1,0:T(8,128)S(1)}, u32[]{:S(2)}, u32[]{:S(2)}) collective-permute-start(f32[8,64,128]{2,1,0:T(8,128)} %bitcast.60), channel_id=1, source_target_pairs={{0,16},{16,0},{32,48},{48,32},{64,80},{80,64},{96,112},{112,96},{1... | collective-permute-start | bytes 786440 | tf_op jit(solution)/shard_map/ppermute | solution.py:308
  24.2 13.8 %collective-permute-start.7 = (f32[64,128]{1,0:T(8,128)S(1)}, f32[64,128]{1,0:T(8,128)S(1)}, u32[]{:S(2)}, u32[]{:S(2)}) collective-permute-start(f32[64,128]{1,0:T(8,128)S(1)} %get-tuple-element.18), channel_id=1, source_target_pairs={{0,224},{16,240},{32,192},{48,208},{64,160},{80,176},{96,128},{112... | collective-permute-start | bytes 98312 | tf_op jit(solution)/shard_map/ppermute | solution.py:308
  27.7 10.3 %collective-permute-start.6 = (f32[64,128]{1,0:T(8,128)S(1)}, f32[64,128]{1,0:T(8,128)S(1)}, u32[]{:S(2)}, u32[]{:S(2)}) collective-permute-start(f32[64,128]{1,0:T(8,128)S(1)} %get-tuple-element.19), channel_id=1, source_target_pairs={{0,192},{16,208},{32,224},{48,240},{64,128},{80,144},{96,160},{112... | collective-permute-start | bytes 98312 | tf_op jit(solution)/shard_map/ppermute | solution.py:308
  29.5 9.0 %collective-permute-start.5 = (f32[64,128]{1,0:T(8,128)S(1)}, f32[64,128]{1,0:T(8,128)S(1)}, u32[]{:S(2)}, u32[]{:S(2)}) collective-permute-start(f32[64,128]{1,0:T(8,128)S(1)} %get-tuple-element.20), channel_id=1, source_target_pairs={{0,160},{16,176},{32,128},{48,144},{64,224},{80,240},{96,192},{112... | collective-permute-start | bytes 98312 | tf_op jit(solution)/shard_map/ppermute | solution.py:308
  34.9 6.9 %collective-permute-start.4 = (f32[64,128]{1,0:T(8,128)S(1)}, f32[64,128]{1,0:T(8,128)S(1)}, u32[]{:S(2)}, u32[]{:S(2)}) collective-permute-start(f32[64,128]{1,0:T(8,128)S(1)} %get-tuple-element.21), channel_id=1, source_target_pairs={{0,128},{16,144},{32,160},{48,176},{64,192},{80,208},{96,224},{112... | collective-permute-start | bytes 98312 | tf_op jit(solution)/shard_map/ppermute | solution.py:308
  34.9 6.9 %collective-permute-start.3 = (f32[64,128]{1,0:T(8,128)S(1)}, f32[64,128]{1,0:T(8,128)S(1)}, u32[]{:S(2)}, u32[]{:S(2)}) collective-permute-start(f32[64,128]{1,0:T(8,128)S(1)} %get-tuple-element.22), channel_id=1, source_target_pairs={{0,96},{16,112},{32,64},{48,80},{64,32},{80,48},{96,0},{112,16},{1... | collective-permute-start | bytes 98312 | tf_op jit(solution)/shard_map/ppermute | solution.py:308
  38.0 3.9 %collective-permute-start.2 = (f32[64,128]{1,0:T(8,128)S(1)}, f32[64,128]{1,0:T(8,128)S(1)}, u32[]{:S(2)}, u32[]{:S(2)}) collective-permute-start(f32[64,128]{1,0:T(8,128)S(1)} %get-tuple-element.23), channel_id=1, source_target_pairs={{0,64},{16,80},{32,96},{48,112},{64,0},{80,16},{96,32},{112,48},{1... | collective-permute-start | bytes 98312 | tf_op jit(solution)/shard_map/ppermute | solution.py:308
  38.0 3.9 %collective-permute-start.1 = (f32[64,128]{1,0:T(8,128)S(1)}, f32[64,128]{1,0:T(8,128)S(1)}, u32[]{:S(2)}, u32[]{:S(2)}) collective-permute-start(f32[64,128]{1,0:T(8,128)S(1)} %get-tuple-element.24), channel_id=1, source_target_pairs={{0,32},{16,48},{32,0},{48,16},{64,96},{80,112},{96,64},{112,80},{1... | collective-permute-start | bytes 98312 | tf_op jit(solution)/shard_map/ppermute | solution.py:308
  42.6 19.8 %all-to-all-start.1 = ((f32[16,16,128]{2,1,0:T(8,128)}), f32[16,16,128]{2,1,0:T(8,128)S(1)}, u32[]{:S(2)}, u32[]{:S(2)}) async-start(f32[16,16,128]{2,1,0:T(8,128)} %get-tuple-element.13), calls=%async_computation.1 | async-start | bytes 262144 | tf_op jit(solution)/shard_map/all_to_all | solution.py:304
  74.2 53.8 %all-to-all-start.3 = ((f32[16,128,128]{2,1,0:T(8,128)}), f32[16,128,128]{2,1,0:T(8,128)S(1)}, u32[]{:S(2)}, u32[]{:S(2)}) async-start(f32[16,128,128]{2,1,0:T(8,128)} %shard_map.98), calls=%async_computation.3 | async-start | bytes 2097152 | tf_op jit(solution)/shard_map/all_to_all | solution.py:304
  80.9 34.9 %collective-permute-start.13 = (f32[128,128]{1,0:T(8,128)S(1)}, f32[128,128]{1,0:T(8,128)S(1)}, u32[]{:S(2)}, u32[]{:S(2)}) collective-permute-start(f32[128,128]{1,0:T(8,128)S(1)} %get-tuple-element.14), channel_id=1, source_target_pairs={{0,224},{16,240},{32,192},{48,208},{64,160},{80,176},{96,128},{112... | collective-permute-start | bytes 196616 | tf_op jit(solution)/shard_map/ppermute | solution.py:308
  83.5 26.8 %collective-permute-start.10 = (f32[128,128]{1,0:T(8,128)S(1)}, f32[128,128]{1,0:T(8,128)S(1)}, u32[]{:S(2)}, u32[]{:S(2)}) collective-permute-start(f32[128,128]{1,0:T(8,128)S(1)} %get-tuple-element.14), channel_id=1, source_target_pairs={{0,128},{16,144},{32,160},{48,176},{64,192},{80,208},{96,224},{112... | collective-permute-start | bytes 196616 | tf_op jit(solution)/shard_map/ppermute | solution.py:308
  86.5 23.8 %collective-permute-start.9 = (f32[128,128]{1,0:T(8,128)S(1)}, f32[128,128]{1,0:T(8,128)S(1)}, u32[]{:S(2)}, u32[]{:S(2)}) collective-permute-start(f32[128,128]{1,0:T(8,128)S(1)} %get-tuple-element.14), channel_id=1, source_target_pairs={{0,64},{16,80},{32,96},{48,112},{64,0},{80,16},{96,32},{112,48},{1... | collective-permute-start | bytes 196616 | tf_op jit(solution)/shard_map/ppermute | solution.py:308
  87.7 23.9 %collective-permute-start.8 = (f32[128,128]{1,0:T(8,128)S(1)}, f32[128,128]{1,0:T(8,128)S(1)}, u32[]{:S(2)}, u32[]{:S(2)}) collective-permute-start(f32[128,128]{1,0:T(8,128)S(1)} %get-tuple-element.14), channel_id=1, source_target_pairs={{0,32},{16,48},{32,0},{48,16},{64,96},{80,112},{96,64},{112,80},{1... | collective-permute-start | bytes 196616 | tf_op jit(solution)/shard_map/ppermute | solution.py:308
  111.6 4.3 %collective-permute-start.12 = (f32[128,128]{1,0:T(8,128)S(1)}, f32[128,128]{1,0:T(8,128)S(1)}, u32[]{:S(2)}, u32[]{:S(2)}) collective-permute-start(f32[128,128]{1,0:T(8,128)S(1)} %collective-permute-done.10), channel_id=1, source_target_pairs={{0,64},{16,80},{32,96},{48,112},{64,0},{80,16},{96,32},{112,48},{1... | collective-permute-start | bytes 196616 | tf_op jit(solution)/shard_map/ppermute | solution.py:308
  114.0 4.4 %collective-permute-start.11 = (f32[2,128,128]{2,1,0:T(8,128)S(1)}, f32[2,128,128]{2,1,0:T(8,128)S(1)}, u32[]{:S(2)}, u32[]{:S(2)}) collective-permute-start(f32[2,128,128]{2,1,0:T(8,128)S(1)} %pad_maximum_fusion.3), channel_id=1, source_target_pairs={{0,32},{16,48},{32,0},{48,16},{64,96},{80,112},{96,64},{112,80},{1... | collective-permute-start | bytes 393224 | tf_op jit(solution)/shard_map/ppermute | solution.py:308
  114.8 12.1 %copy-start.4 = (f32[8,128,128]{2,1,0:T(8,128)S(1)}, f32[8,128,128]{2,1,0:T(8,128)}, u32[]{:S(2)}) copy-start(f32[8,128,128]{2,1,0:T(8,128)} %alda_ref.1) | copy-start | bytes 1572868
  114.8 12.2 %copy-start.5 = (f32[8,128,128]{2,1,0:T(8,128)S(1)}, f32[8,128,128]{2,1,0:T(8,128)}, u32[]{:S(2)}) copy-start(f32[8,128,128]{2,1,0:T(8,128)} %local_ref.1) | copy-start | bytes 1572868
  114.8 5.9 %collective-permute-start.14 = (f32[4,128,128]{2,1,0:T(8,128)S(1)}, f32[4,128,128]{2,1,0:T(8,128)S(1)}, u32[]{:S(2)}, u32[]{:S(2)}) collective-permute-start(f32[4,128,128]{2,1,0:T(8,128)S(1)} %pad_maximum_fusion.1), channel_id=1, source_target_pairs={{0,16},{16,0},{32,48},{48,32},{64,80},{80,64},{96,112},{112,96},{1... | collective-permute-start | bytes 786440 | tf_op jit(solution)/shard_map/ppermute | solution.py:308
  118.5 8.3 %collective-permute-start.15 = (f32[4,128,128]{2,1,0:T(8,128)S(1)}, f32[4,128,128]{2,1,0:T(8,128)S(1)}, u32[]{:S(2)}, u32[]{:S(2)}) collective-permute-start(f32[4,128,128]{2,1,0:T(8,128)S(1)} %pad_maximum_fusion.2), channel_id=1, source_target_pairs={{0,16},{16,0},{32,48},{48,32},{64,80},{80,64},{96,112},{112,96},{1... | collective-permute-start | bytes 786440 | tf_op jit(solution)/shard_map/ppermute | solution.py:308
  131.8 33.6 %copy-start.6 = (bf16[2,256,256]{2,1,0:T(8,128)(2,1)S(1)}, bf16[2,256,256]{2,1,0:T(8,128)(2,1)}, u32[]{:S(2)}) copy-start(bf16[2,256,256]{2,1,0:T(8,128)(2,1)} %constant.62.clone.x_ref) | copy-start | bytes 786436
  (2 other events, 24.3 us)

commit v3 on v2

--- a/solution.py
+++ b/solution.py
@@ -170,14 +170,17 @@
     out_ref[...] = product(pair(up_ref), split(turned)).reshape(parts, share, length)
 
 
-def spread_kernel(pieces_ref, out_ref):
+def spread_kernel(pieces_ref, down_ref, out_ref):
     share = pieces_ref.shape[0] // out_ref.shape[0]
+    tiles = []
     for part in range(2):
-        for x in range(share):
-            block = pieces_ref[pl.ds(part * share + x, share, stride=2 * share), :]
-            rows = pl.ds((part * share + x) * share, share)
-            for i in range(out_ref.shape[0]):
-                out_ref[i, rows, :] = block
+        rows = [
+            pieces_ref[pl.ds(part * share + x, share, stride=2 * share), :] for x in range(share)
+        ]
+        tiles.append(jnp.concatenate(rows, axis=0))
+    value = parts_down(product(split(jnp.concatenate(tiles, axis=1)), pair(down_ref)))
+    for i in range(out_ref.shape[0]):
+        out_ref[i] = value
 
 
 def back(blocks, up_ref, down_ref, length):
@@ -229,12 +232,12 @@
                 [potential_ref[:, part, x].reshape(length, length) for part in range(2)], axis=0
             )
         )
-    value = back(jnp.concatenate(columns, axis=1), up_ref, down_ref, length)
+    value = product(pair(up_ref), split(jnp.concatenate(columns, axis=1)))
     fields = []
     for x in range(rows):
         orbital = orbital_ref[0, x].astype(WIDE)
         for k in range(2):
-            block = value[x * length : (x + 1) * length, k * length : (k + 1) * length]
+            block = value[k * length : (k + 1) * length, x * length : (x + 1) * length]
             fields.append(block * orbital + base_ref[k, x])
     table = (up_ref[0, :length, :], up_ref[1, :length, :])
     turned = product(split(jnp.concatenate(fields, axis=0)), table)
@@ -378,7 +381,9 @@
             away[mask] = group[i]
     near = jnp.stack([held[mask] for mask in range(0, parts, 2)])
     far = jnp.stack([away[mask] for mask in range(0, parts, 2)])
-    potential = call(spread_kernel, (parts, 2 * points, length))(lines)
+    potential = call(spread_kernel, (parts, 2 * points, length))(
+        lines, tables["down"]
+    )
     potential = exchange(potential, "band").reshape(parts, 2, share, share, length)
     base = call(
         base_kernel,

time: 168 us -> 168 us (level)
  no operation moved by 1% of the time
where the time goes in v3:
time: 168 us; the launch traced here: 167 us
  starting transfers between devices  56.1 us (33%)
  waiting for transfers between devices  51.2 us (30%)
  blocking collectives  43.8 us (26%)
  Pallas kernels  13.2 us (8%)
  between operations  1.71 us (1%)
    all_to_all x2, blocking collectives, exchange(): return lax.all_to_all(array, axis, split_axis=0, concat_axis=0, tiled=True)  43.8 us
    ppermute x16, waiting for transfers between devices, partner(): lax.ppermute(array, 'band', [(i, i ^ mask) for i in range(lax.axis_size('...  43.8 us
    all_to_all x3, starting transfers between devices, exchange(): return lax.all_to_all(array, axis, split_axis=0, concat_axis=0, tiled=True)  28.4 us
    ppermute x16, starting transfers between devices, partner(): lax.ppermute(array, 'band', [(i, i ^ mask) for i in range(lax.axis_size('...  27.7 us
    all_to_all x3, waiting for transfers between devices, exchange(): return lax.all_to_all(array, axis, split_axis=0, concat_axis=0, tiled=True)  7.48 us
    pallas_call x1, Pallas kernels, per_device(): call(density_kernel, [some, some, (parts, 2, half, share, length)], grant...  4.17 us
    pallas_call x1, Pallas kernels, per_device(): call(field_kernel, (parts, 2, 2, share, share, length), grid=steps, in_sp...  3.57 us
  transfers between devices with their start and end apart: 19, of which 9 were waited for; matrix products, arithmetic and copies ran while one was open for 1% of the time, Pallas kernels for 1%

profile of v3, /device:TPU:1, one launch (start us, length us, event | category | flops | bytes accessed | tf_op | source)
XLA Modules:
  0.0 167.5 jit_solution(17292528353630705713)
XLA Ops:
  0.6 4.2 %shard_map.95 = (f32[8,2,4,8,128]{4,3,2,1,0:T(8,128)}, f32[8,2,4,8,128]{4,3,2,1,0:T(8,128)}, f32[16,2,4,8,128]{4,3,2,1,0:T(8,128)}) custom-call(s32[1]{0:T(128)} %bitcast.me_ref, bf16[1,8,128,128]{3,2,1,0:T(8,128)(2,1)} %orbital_ref.3, bf16[2,1,8,128,128]{4,3,2,1,0:T(8,128)(2,1)} %trial_ref.1, bf16[2,256,256]{2,1,0:T(8,128)(2,1)} %constant.61.clone.up_in.up_ref, ...), custom_call_target="tpu_custom_call" | custom-call | tf_op jit(solution)/shard_map/pallas_call | solution.py:339
  4.8 10.3 %all-to-all-start = ((f32[16,64,128]{2,1,0:T(8,128)}), f32[16,64,128]{2,1,0:T(8,128)S(1)}, u32[]{:S(2)}, u32[]{:S(2)}) async-start(f32[16,64,128]{2,1,0:T(8,128)} %bitcast.51), calls=%async_computation | async-start | bytes 1048576 | tf_op jit(solution)/shard_map/all_to_all | solution.py:307
  15.1 1.4 collective-permute-start
  16.5 6.7 %collective-permute-done = f32[8,64,128]{2,1,0:T(8,128)S(1)} collective-permute-done((f32[8,64,128]{2,1,0:T(8,128)}, f32[8,64,128]{2,1,0:T(8,128)S(1)}, u32[]{:S(2)}, u32[]{:S(2)}) %collective-permute-start) | collective-permute-done | bytes 262176 | tf_op jit(solution)/shard_map/ppermute | solution.py:311
  24.2 3.5 %collective-permute-start.7 = (f32[64,128]{1,0:T(8,128)S(1)}, f32[64,128]{1,0:T(8,128)S(1)}, u32[]{:S(2)}, u32[]{:S(2)}) collective-permute-start(f32[64,128]{1,0:T(8,128)S(1)} %get-tuple-element.18), channel_id=1, source_target_pairs={{0,224},{16,240},{32,192},{48,208},{64,160},{80,176},{96,128},{112... | collective-permute-start | bytes 98312 | tf_op jit(solution)/shard_map/ppermute | solution.py:311
  27.7 1.8 %collective-permute-start.6 = (f32[64,128]{1,0:T(8,128)S(1)}, f32[64,128]{1,0:T(8,128)S(1)}, u32[]{:S(2)}, u32[]{:S(2)}) collective-permute-start(f32[64,128]{1,0:T(8,128)S(1)} %get-tuple-element.19), channel_id=1, source_target_pairs={{0,192},{16,208},{32,224},{48,240},{64,128},{80,144},{96,160},{112... | collective-permute-start | bytes 98312 | tf_op jit(solution)/shard_map/ppermute | solution.py:311
  29.5 5.4 %collective-permute-start.5 = (f32[64,128]{1,0:T(8,128)S(1)}, f32[64,128]{1,0:T(8,128)S(1)}, u32[]{:S(2)}, u32[]{:S(2)}) collective-permute-start(f32[64,128]{1,0:T(8,128)S(1)} %get-tuple-element.20), channel_id=1, source_target_pairs={{0,160},{16,176},{32,128},{48,144},{64,224},{80,240},{96,192},{112... | collective-permute-start | bytes 98312 | tf_op jit(solution)/shard_map/ppermute | solution.py:311
  34.9 3.1 %collective-permute-start.3 = (f32[64,128]{1,0:T(8,128)S(1)}, f32[64,128]{1,0:T(8,128)S(1)}, u32[]{:S(2)}, u32[]{:S(2)}) collective-permute-start(f32[64,128]{1,0:T(8,128)S(1)} %get-tuple-element.22), channel_id=1, source_target_pairs={{0,96},{16,112},{32,64},{48,80},{64,32},{80,48},{96,0},{112,16},{1... | collective-permute-start | bytes 98312 | tf_op jit(solution)/shard_map/ppermute | solution.py:311
  38.5 3.4 %collective-permute-done.4.refs_4_ = f32[64,128]{1,0:T(8,128)S(1)} collective-permute-done((f32[64,128]{1,0:T(8,128)S(1)}, f32[64,128]{1,0:T(8,128)S(1)}, u32[]{:S(2)}, u32[]{:S(2)}) %collective-permute-start.4) | collective-permute-done | bytes 32800 | tf_op jit(solution)/shard_map/ppermute | solution.py:311
  42.6 12.1 %all-to-all-start.1 = ((f32[16,16,128]{2,1,0:T(8,128)}), f32[16,16,128]{2,1,0:T(8,128)S(1)}, u32[]{:S(2)}, u32[]{:S(2)}) async-start(f32[16,16,128]{2,1,0:T(8,128)} %get-tuple-element.13), calls=%async_computation.1 | async-start | bytes 262144 | tf_op jit(solution)/shard_map/all_to_all | solution.py:307
  54.9 7.5 %all-to-all-done.1.pieces_ref = f32[16,16,128]{2,1,0:T(8,128)S(1)} async-done(((f32[16,16,128]{2,1,0:T(8,128)}), f32[16,16,128]{2,1,0:T(8,128)S(1)}, u32[]{:S(2)}, u32[]{:S(2)}) %all-to-all-start.1) | async-done | bytes 131104 | tf_op jit(solution)/shard_map/all_to_all | solution.py:307
  62.9 10.3 %all_to_all.25 = f32[16,8,128]{2,1,0:T(8,128)S(1)} all-to-all(f32[16,8,128]{2,1,0:T(8,128)S(1)} %shard_map.97), channel_id=1, replica_groups=mesh['band'=16,'grid'=16] {'grid'}, dimensions={0} | all-to-all | bytes 131072 | tf_op jit(solution)/shard_map/all_to_all | solution.py:307
  73.1 1.3 shard_map.98
  74.4 6.0 %all-to-all-start.3 = ((f32[16,128,128]{2,1,0:T(8,128)}), f32[16,128,128]{2,1,0:T(8,128)S(1)}, u32[]{:S(2)}, u32[]{:S(2)}) async-start(f32[16,128,128]{2,1,0:T(8,128)} %shard_map.98), calls=%async_computation.3 | async-start | bytes 2097152 | tf_op jit(solution)/shard_map/all_to_all | solution.py:307
  81.1 2.7 %collective-permute-start.13 = (f32[128,128]{1,0:T(8,128)S(1)}, f32[128,128]{1,0:T(8,128)S(1)}, u32[]{:S(2)}, u32[]{:S(2)}) collective-permute-start(f32[128,128]{1,0:T(8,128)S(1)} %get-tuple-element.14), channel_id=1, source_target_pairs={{0,224},{16,240},{32,192},{48,208},{64,160},{80,176},{96,128},{112... | collective-permute-start | bytes 196616 | tf_op jit(solution)/shard_map/ppermute | solution.py:311
  83.8 3.0 %collective-permute-start.10 = (f32[128,128]{1,0:T(8,128)S(1)}, f32[128,128]{1,0:T(8,128)S(1)}, u32[]{:S(2)}, u32[]{:S(2)}) collective-permute-start(f32[128,128]{1,0:T(8,128)S(1)} %get-tuple-element.14), channel_id=1, source_target_pairs={{0,128},{16,144},{32,160},{48,176},{64,192},{80,208},{96,224},{112... | collective-permute-start | bytes 196616 | tf_op jit(solution)/shard_map/ppermute | solution.py:311
  87.9 22.7 %collective-permute-done.10 = f32[128,128]{1,0:T(8,128)S(1)} collective-permute-done((f32[128,128]{1,0:T(8,128)S(1)}, f32[128,128]{1,0:T(8,128)S(1)}, u32[]{:S(2)}, u32[]{:S(2)}) %collective-permute-start.10) | collective-permute-done | bytes 65568 | tf_op jit(solution)/shard_map/ppermute | solution.py:311
  110.6 1.2 collective-permute-done.8
  111.8 2.5 %collective-permute-start.12 = (f32[128,128]{1,0:T(8,128)S(1)}, f32[128,128]{1,0:T(8,128)S(1)}, u32[]{:S(2)}, u32[]{:S(2)}) collective-permute-start(f32[128,128]{1,0:T(8,128)S(1)} %collective-permute-done.10), channel_id=1, source_target_pairs={{0,64},{16,80},{32,96},{48,112},{64,0},{80,16},{96,32},{112,48},{1... | collective-permute-start | bytes 196616 | tf_op jit(solution)/shard_map/ppermute | solution.py:311
  116.1 2.6 %collective-permute-done.11 = f32[2,128,128]{2,1,0:T(8,128)S(1)} collective-permute-done((f32[2,128,128]{2,1,0:T(8,128)S(1)}, f32[2,128,128]{2,1,0:T(8,128)S(1)}, u32[]{:S(2)}, u32[]{:S(2)}) %collective-permute-start.11) | collective-permute-done | bytes 131104 | tf_op jit(solution)/shard_map/ppermute | solution.py:311
  120.9 6.1 %collective-permute-done.15 = f32[4,128,128]{2,1,0:T(8,128)S(1)} collective-permute-done((f32[4,128,128]{2,1,0:T(8,128)S(1)}, f32[4,128,128]{2,1,0:T(8,128)S(1)}, u32[]{:S(2)}, u32[]{:S(2)}) %collective-permute-start.15) | collective-permute-done | bytes 262176 | tf_op jit(solution)/shard_map/ppermute | solution.py:311
  128.2 3.6 %shard_map.100 = f32[16,2,2,8,8,128]{5,4,3,2,1,0:T(8,128)S(1)} custom-call(f32[16,2,8,8,128]{4,3,2,1,0:T(8,128)S(1)} %bitcast.40, bf16[1,8,128,128]{3,2,1,0:T(8,128)(2,1)S(1)} %copy-done.2, f32[2,8,128,128]{3,2,1,0:T(8,128)S(1)} %shard_map.99.base_ref, bf16[2,256,256]{2,1,0:T(8,128)(2,1)S(1)} %copy-done.1, bf16[2,256,256]{2,1,0:T(8,128)(2,1)S(1)} %copy-done), custom_call_target="tpu_custom_call" | custom-call | tf_op jit(solution)/shard_map/pallas_call | solution.py:409
  131.8 33.6 %all_to_all.26.pieces_ref = f32[16,256,128]{2,1,0:T(8,128)S(1)} all-to-all(f32[16,256,128]{2,1,0:T(8,128)S(1)} %bitcast.39), channel_id=1, replica_groups=mesh['band'=16,'grid'=16] {'grid'}, dimensions={0} | all-to-all | bytes 4194304 | tf_op jit(solution)/shard_map/all_to_all | solution.py:307
  165.4 1.9 %shard_map.101 = (f32[2,1,8,128,128]{4,3,2,1,0:T(8,128)}, f32[2,1,8,128,128]{4,3,2,1,0:T(8,128)}) custom-call(f32[16,256,128]{2,1,0:T(8,128)S(1)} %all_to_all.26.pieces_ref, bf16[2,256,256]{2,1,0:T(8,128)(2,1)S(1)} %copy-done.6), custom_call_target="tpu_custom_call" | custom-call | tf_op jit(solution)/shard_map/pallas_call | solution.py:422
  (60 shorter events, 9.2 us)
Async XLA Ops:
  4.8 50.1 %copy-start.1 = (bf16[2,256,256]{2,1,0:T(8,128)(2,1)S(1)}, bf16[2,256,256]{2,1,0:T(8,128)(2,1)}, u32[]{:S(2)}) copy-start(bf16[2,256,256]{2,1,0:T(8,128)(2,1)} %constant.61.clone.up_in.up_ref) | copy-start | bytes 786436
  4.8 57.6 %copy-start = (bf16[2,256,256]{2,1,0:T(8,128)(2,1)S(1)}, bf16[2,256,256]{2,1,0:T(8,128)(2,1)}, u32[]{:S(2)}) copy-start(bf16[2,256,256]{2,1,0:T(8,128)(2,1)} %constant.60.clone.down_in.down_ref) | copy-start | bytes 786436
  4.8 37.0 %all-to-all-start = ((f32[16,64,128]{2,1,0:T(8,128)}), f32[16,64,128]{2,1,0:T(8,128)S(1)}, u32[]{:S(2)}, u32[]{:S(2)}) async-start(f32[16,64,128]{2,1,0:T(8,128)} %bitcast.51), calls=%async_computation | async-start | bytes 1048576 | tf_op jit(solution)/shard_map/all_to_all | solution.py:307
  15.1 8.1 %collective-permute-start = (f32[8,64,128]{2,1,0:T(8,128)}, f32[8,64,128]{2,1,0:T(8,128)S(1)}, u32[]{:S(2)}, u32[]{:S(2)}) collective-permute-start(f32[8,64,128]{2,1,0:T(8,128)} %bitcast.60), channel_id=1, source_target_pairs={{0,16},{16,0},{32,48},{48,32},{64,80},{80,64},{96,112},{112,96},{1... | collective-permute-start | bytes 786440 | tf_op jit(solution)/shard_map/ppermute | solution.py:311
  24.2 13.8 %collective-permute-start.7 = (f32[64,128]{1,0:T(8,128)S(1)}, f32[64,128]{1,0:T(8,128)S(1)}, u32[]{:S(2)}, u32[]{:S(2)}) collective-permute-start(f32[64,128]{1,0:T(8,128)S(1)} %get-tuple-element.18), channel_id=1, source_target_pairs={{0,224},{16,240},{32,192},{48,208},{64,160},{80,176},{96,128},{112... | collective-permute-start | bytes 98312 | tf_op jit(solution)/shard_map/ppermute | solution.py:311
  27.7 10.3 %collective-permute-start.6 = (f32[64,128]{1,0:T(8,128)S(1)}, f32[64,128]{1,0:T(8,128)S(1)}, u32[]{:S(2)}, u32[]{:S(2)}) collective-permute-start(f32[64,128]{1,0:T(8,128)S(1)} %get-tuple-element.19), channel_id=1, source_target_pairs={{0,192},{16,208},{32,224},{48,240},{64,128},{80,144},{96,160},{112... | collective-permute-start | bytes 98312 | tf_op jit(solution)/shard_map/ppermute | solution.py:311
  29.5 9.0 %collective-permute-start.5 = (f32[64,128]{1,0:T(8,128)S(1)}, f32[64,128]{1,0:T(8,128)S(1)}, u32[]{:S(2)}, u32[]{:S(2)}) collective-permute-start(f32[64,128]{1,0:T(8,128)S(1)} %get-tuple-element.20), channel_id=1, source_target_pairs={{0,160},{16,176},{32,128},{48,144},{64,224},{80,240},{96,192},{112... | collective-permute-start | bytes 98312 | tf_op jit(solution)/shard_map/ppermute | solution.py:311
  34.9 6.9 %collective-permute-start.4 = (f32[64,128]{1,0:T(8,128)S(1)}, f32[64,128]{1,0:T(8,128)S(1)}, u32[]{:S(2)}, u32[]{:S(2)}) collective-permute-start(f32[64,128]{1,0:T(8,128)S(1)} %get-tuple-element.21), channel_id=1, source_target_pairs={{0,128},{16,144},{32,160},{48,176},{64,192},{80,208},{96,224},{112... | collective-permute-start | bytes 98312 | tf_op jit(solution)/shard_map/ppermute | solution.py:311
  34.9 6.9 %collective-permute-start.3 = (f32[64,128]{1,0:T(8,128)S(1)}, f32[64,128]{1,0:T(8,128)S(1)}, u32[]{:S(2)}, u32[]{:S(2)}) collective-permute-start(f32[64,128]{1,0:T(8,128)S(1)} %get-tuple-element.22), channel_id=1, source_target_pairs={{0,96},{16,112},{32,64},{48,80},{64,32},{80,48},{96,0},{112,16},{1... | collective-permute-start | bytes 98312 | tf_op jit(solution)/shard_map/ppermute | solution.py:311
  38.0 3.9 %collective-permute-start.2 = (f32[64,128]{1,0:T(8,128)S(1)}, f32[64,128]{1,0:T(8,128)S(1)}, u32[]{:S(2)}, u32[]{:S(2)}) collective-permute-start(f32[64,128]{1,0:T(8,128)S(1)} %get-tuple-element.23), channel_id=1, source_target_pairs={{0,64},{16,80},{32,96},{48,112},{64,0},{80,16},{96,32},{112,48},{1... | collective-permute-start | bytes 98312 | tf_op jit(solution)/shard_map/ppermute | solution.py:311
  38.0 3.9 %collective-permute-start.1 = (f32[64,128]{1,0:T(8,128)S(1)}, f32[64,128]{1,0:T(8,128)S(1)}, u32[]{:S(2)}, u32[]{:S(2)}) collective-permute-start(f32[64,128]{1,0:T(8,128)S(1)} %get-tuple-element.24), channel_id=1, source_target_pairs={{0,32},{16,48},{32,0},{48,16},{64,96},{80,112},{96,64},{112,80},{1... | collective-permute-start | bytes 98312 | tf_op jit(solution)/shard_map/ppermute | solution.py:311
  42.6 19.8 %all-to-all-start.1 = ((f32[16,16,128]{2,1,0:T(8,128)}), f32[16,16,128]{2,1,0:T(8,128)S(1)}, u32[]{:S(2)}, u32[]{:S(2)}) async-start(f32[16,16,128]{2,1,0:T(8,128)} %get-tuple-element.13), calls=%async_computation.1 | async-start | bytes 262144 | tf_op jit(solution)/shard_map/all_to_all | solution.py:307
  74.4 53.8 %all-to-all-start.3 = ((f32[16,128,128]{2,1,0:T(8,128)}), f32[16,128,128]{2,1,0:T(8,128)S(1)}, u32[]{:S(2)}, u32[]{:S(2)}) async-start(f32[16,128,128]{2,1,0:T(8,128)} %shard_map.98), calls=%async_computation.3 | async-start | bytes 2097152 | tf_op jit(solution)/shard_map/all_to_all | solution.py:307
  81.1 34.9 %collective-permute-start.13 = (f32[128,128]{1,0:T(8,128)S(1)}, f32[128,128]{1,0:T(8,128)S(1)}, u32[]{:S(2)}, u32[]{:S(2)}) collective-permute-start(f32[128,128]{1,0:T(8,128)S(1)} %get-tuple-element.14), channel_id=1, source_target_pairs={{0,224},{16,240},{32,192},{48,208},{64,160},{80,176},{96,128},{112... | collective-permute-start | bytes 196616 | tf_op jit(solution)/shard_map/ppermute | solution.py:311
  83.8 26.8 %collective-permute-start.10 = (f32[128,128]{1,0:T(8,128)S(1)}, f32[128,128]{1,0:T(8,128)S(1)}, u32[]{:S(2)}, u32[]{:S(2)}) collective-permute-start(f32[128,128]{1,0:T(8,128)S(1)} %get-tuple-element.14), channel_id=1, source_target_pairs={{0,128},{16,144},{32,160},{48,176},{64,192},{80,208},{96,224},{112... | collective-permute-start | bytes 196616 | tf_op jit(solution)/shard_map/ppermute | solution.py:311
  86.7 23.8 %collective-permute-start.9 = (f32[128,128]{1,0:T(8,128)S(1)}, f32[128,128]{1,0:T(8,128)S(1)}, u32[]{:S(2)}, u32[]{:S(2)}) collective-permute-start(f32[128,128]{1,0:T(8,128)S(1)} %get-tuple-element.14), channel_id=1, source_target_pairs={{0,64},{16,80},{32,96},{48,112},{64,0},{80,16},{96,32},{112,48},{1... | collective-permute-start | bytes 196616 | tf_op jit(solution)/shard_map/ppermute | solution.py:311
  87.9 23.9 %collective-permute-start.8 = (f32[128,128]{1,0:T(8,128)S(1)}, f32[128,128]{1,0:T(8,128)S(1)}, u32[]{:S(2)}, u32[]{:S(2)}) collective-permute-start(f32[128,128]{1,0:T(8,128)S(1)} %get-tuple-element.14), channel_id=1, source_target_pairs={{0,32},{16,48},{32,0},{48,16},{64,96},{80,112},{96,64},{112,80},{1... | collective-permute-start | bytes 196616 | tf_op jit(solution)/shard_map/ppermute | solution.py:311
  111.8 4.3 %collective-permute-start.12 = (f32[128,128]{1,0:T(8,128)S(1)}, f32[128,128]{1,0:T(8,128)S(1)}, u32[]{:S(2)}, u32[]{:S(2)}) collective-permute-start(f32[128,128]{1,0:T(8,128)S(1)} %collective-permute-done.10), channel_id=1, source_target_pairs={{0,64},{16,80},{32,96},{48,112},{64,0},{80,16},{96,32},{112,48},{1... | collective-permute-start | bytes 196616 | tf_op jit(solution)/shard_map/ppermute | solution.py:311
  114.3 4.4 %collective-permute-start.11 = (f32[2,128,128]{2,1,0:T(8,128)S(1)}, f32[2,128,128]{2,1,0:T(8,128)S(1)}, u32[]{:S(2)}, u32[]{:S(2)}) collective-permute-start(f32[2,128,128]{2,1,0:T(8,128)S(1)} %pad_maximum_fusion.3), channel_id=1, source_target_pairs={{0,32},{16,48},{32,0},{48,16},{64,96},{80,112},{96,64},{112,80},{1... | collective-permute-start | bytes 393224 | tf_op jit(solution)/shard_map/ppermute | solution.py:311
  115.0 12.1 %copy-start.4 = (f32[8,128,128]{2,1,0:T(8,128)S(1)}, f32[8,128,128]{2,1,0:T(8,128)}, u32[]{:S(2)}) copy-start(f32[8,128,128]{2,1,0:T(8,128)} %alda_ref.1) | copy-start | bytes 1572868
  115.0 12.2 %copy-start.5 = (f32[8,128,128]{2,1,0:T(8,128)S(1)}, f32[8,128,128]{2,1,0:T(8,128)}, u32[]{:S(2)}) copy-start(f32[8,128,128]{2,1,0:T(8,128)} %local_ref.1) | copy-start | bytes 1572868
  115.0 5.9 %collective-permute-start.14 = (f32[4,128,128]{2,1,0:T(8,128)S(1)}, f32[4,128,128]{2,1,0:T(8,128)S(1)}, u32[]{:S(2)}, u32[]{:S(2)}) collective-permute-start(f32[4,128,128]{2,1,0:T(8,128)S(1)} %pad_maximum_fusion.1), channel_id=1, source_target_pairs={{0,16},{16,0},{32,48},{48,32},{64,80},{80,64},{96,112},{112,96},{1... | collective-permute-start | bytes 786440 | tf_op jit(solution)/shard_map/ppermute | solution.py:311
  118.7 8.3 %collective-permute-start.15 = (f32[4,128,128]{2,1,0:T(8,128)S(1)}, f32[4,128,128]{2,1,0:T(8,128)S(1)}, u32[]{:S(2)}, u32[]{:S(2)}) collective-permute-start(f32[4,128,128]{2,1,0:T(8,128)S(1)} %pad_maximum_fusion.2), channel_id=1, source_target_pairs={{0,16},{16,0},{32,48},{48,32},{64,80},{80,64},{96,112},{112,96},{1... | collective-permute-start | bytes 786440 | tf_op jit(solution)/shard_map/ppermute | solution.py:311
  131.8 33.6 %copy-start.6 = (bf16[2,256,256]{2,1,0:T(8,128)(2,1)S(1)}, bf16[2,256,256]{2,1,0:T(8,128)(2,1)}, u32[]{:S(2)}) copy-start(bf16[2,256,256]{2,1,0:T(8,128)(2,1)} %constant.62.clone.x_ref) | copy-start | bytes 786436
  (2 other events, 24.3 us)

commit v4 on v2

--- a/solution.py
+++ b/solution.py
@@ -105,8 +105,7 @@
     ]
     for copy in (tables[0], orbitals[0], trials[0], tables[1], orbitals[1], trials[1]):
         copy.start()
-    for copy in tables:
-        copy.wait()
+    tables[0].wait()
     for i in range(2):
         orbitals[i].wait()
         trials[i].wait()
@@ -120,6 +119,8 @@
             )
         turned = product(split(jnp.concatenate(values, axis=0)), pair(up_ref))
         columns = [parts_down(turned[x * length : (x + 1) * length]) for x in range(half)]
+        if i == 0:
+            tables[1].wait()
         turned = product(pair(down_ref), split(jnp.concatenate(columns, axis=1)))
         for x in range(half):
             for part in range(2):
@@ -251,7 +252,7 @@
     length = real_ref.shape[-1]
     share = real_ref.shape[2]
     table = pair(x_ref)
-    group = share // 2
+    group = share // 4
     copies = []
     for k in range(2):
         for b in range(share):
@@ -422,7 +423,7 @@
             scratch_shapes=[
                 pltpu.VMEM(shape, WIDE),
                 pltpu.VMEM(shape, WIDE),
-                pltpu.SemaphoreType.DMA((8,)),
+                pltpu.SemaphoreType.DMA((16,)),
             ],
         )(received, tables["last"])
     )

time: 168 us -> 168 us (level)
  no operation moved by 1% of the time
where the time goes in v4:
time: 168 us; the launch traced here: 167 us
  starting transfers between devices  56.1 us (33%)
  waiting for transfers between devices  51.2 us (30%)
  blocking collectives  43.8 us (26%)
  Pallas kernels  13.1 us (8%)
  between operations  1.71 us (1%)
    all_to_all x2, blocking collectives, exchange(): return lax.all_to_all(array, axis, split_axis=0, concat_axis=0, tiled=True)  43.8 us
    ppermute x16, waiting for transfers between devices, partner(): lax.ppermute(array, 'band', [(i, i ^ mask) for i in range(lax.axis_size('...  43.8 us
    all_to_all x3, starting transfers between devices, exchange(): return lax.all_to_all(array, axis, split_axis=0, concat_axis=0, tiled=True)  28.4 us
    ppermute x16, starting transfers between devices, partner(): lax.ppermute(array, 'band', [(i, i ^ mask) for i in range(lax.axis_size('...  27.7 us
    all_to_all x3, waiting for transfers between devices, exchange(): return lax.all_to_all(array, axis, split_axis=0, concat_axis=0, tiled=True)  7.48 us
    pallas_call x1, Pallas kernels, per_device(): call(density_kernel, [some, some, (parts, 2, half, share, length)], grant...  4.13 us
    pallas_call x1, Pallas kernels, per_device(): call(field_kernel, (parts, 2, 2, share, share, length), grid=steps, in_sp...  3.78 us
  transfers between devices with their start and end apart: 19, of which 9 were waited for; matrix products, arithmetic and copies ran while one was open for 1% of the time, Pallas kernels for 1%

profile of v4, /device:TPU:1, one launch (start us, length us, event | category | flops | bytes accessed | tf_op | source)
XLA Modules:
  0.0 167.4 jit_solution(11052908484578441222)
XLA Ops:
  0.6 4.1 %shard_map.95 = (f32[8,2,4,8,128]{4,3,2,1,0:T(8,128)}, f32[8,2,4,8,128]{4,3,2,1,0:T(8,128)}, f32[16,2,4,8,128]{4,3,2,1,0:T(8,128)}) custom-call(s32[1]{0:T(128)} %bitcast.me_ref, bf16[1,8,128,128]{3,2,1,0:T(8,128)(2,1)} %orbital_ref.3, bf16[2,1,8,128,128]{4,3,2,1,0:T(8,128)(2,1)} %trial_ref.1, bf16[2,256,256]{2,1,0:T(8,128)(2,1)} %constant.61.clone.up_in.up_ref, ...), custom_call_target="tpu_custom_call" | custom-call | tf_op jit(solution)/shard_map/pallas_call | solution.py:337
  4.8 10.3 %all-to-all-start = ((f32[16,64,128]{2,1,0:T(8,128)}), f32[16,64,128]{2,1,0:T(8,128)S(1)}, u32[]{:S(2)}, u32[]{:S(2)}) async-start(f32[16,64,128]{2,1,0:T(8,128)} %bitcast.51), calls=%async_computation | async-start | bytes 1048576 | tf_op jit(solution)/shard_map/all_to_all | solution.py:305
  15.1 1.4 collective-permute-start
  16.4 6.7 %collective-permute-done = f32[8,64,128]{2,1,0:T(8,128)S(1)} collective-permute-done((f32[8,64,128]{2,1,0:T(8,128)}, f32[8,64,128]{2,1,0:T(8,128)S(1)}, u32[]{:S(2)}, u32[]{:S(2)}) %collective-permute-start) | collective-permute-done | bytes 262176 | tf_op jit(solution)/shard_map/ppermute | solution.py:309
  24.2 3.5 %collective-permute-start.7 = (f32[64,128]{1,0:T(8,128)S(1)}, f32[64,128]{1,0:T(8,128)S(1)}, u32[]{:S(2)}, u32[]{:S(2)}) collective-permute-start(f32[64,128]{1,0:T(8,128)S(1)} %get-tuple-element.18), channel_id=1, source_target_pairs={{0,224},{16,240},{32,192},{48,208},{64,160},{80,176},{96,128},{112... | collective-permute-start | bytes 98312 | tf_op jit(solution)/shard_map/ppermute | solution.py:309
  27.7 1.8 %collective-permute-start.6 = (f32[64,128]{1,0:T(8,128)S(1)}, f32[64,128]{1,0:T(8,128)S(1)}, u32[]{:S(2)}, u32[]{:S(2)}) collective-permute-start(f32[64,128]{1,0:T(8,128)S(1)} %get-tuple-element.19), channel_id=1, source_target_pairs={{0,192},{16,208},{32,224},{48,240},{64,128},{80,144},{96,160},{112... | collective-permute-start | bytes 98312 | tf_op jit(solution)/shard_map/ppermute | solution.py:309
  29.5 5.4 %collective-permute-start.5 = (f32[64,128]{1,0:T(8,128)S(1)}, f32[64,128]{1,0:T(8,128)S(1)}, u32[]{:S(2)}, u32[]{:S(2)}) collective-permute-start(f32[64,128]{1,0:T(8,128)S(1)} %get-tuple-element.20), channel_id=1, source_target_pairs={{0,160},{16,176},{32,128},{48,144},{64,224},{80,240},{96,192},{112... | collective-permute-start | bytes 98312 | tf_op jit(solution)/shard_map/ppermute | solution.py:309
  34.9 3.1 %collective-permute-start.3 = (f32[64,128]{1,0:T(8,128)S(1)}, f32[64,128]{1,0:T(8,128)S(1)}, u32[]{:S(2)}, u32[]{:S(2)}) collective-permute-start(f32[64,128]{1,0:T(8,128)S(1)} %get-tuple-element.22), channel_id=1, source_target_pairs={{0,96},{16,112},{32,64},{48,80},{64,32},{80,48},{96,0},{112,16},{1... | collective-permute-start | bytes 98312 | tf_op jit(solution)/shard_map/ppermute | solution.py:309
  38.5 3.4 %collective-permute-done.4.refs_4_ = f32[64,128]{1,0:T(8,128)S(1)} collective-permute-done((f32[64,128]{1,0:T(8,128)S(1)}, f32[64,128]{1,0:T(8,128)S(1)}, u32[]{:S(2)}, u32[]{:S(2)}) %collective-permute-start.4) | collective-permute-done | bytes 32800 | tf_op jit(solution)/shard_map/ppermute | solution.py:309
  42.6 12.1 %all-to-all-start.1 = ((f32[16,16,128]{2,1,0:T(8,128)}), f32[16,16,128]{2,1,0:T(8,128)S(1)}, u32[]{:S(2)}, u32[]{:S(2)}) async-start(f32[16,16,128]{2,1,0:T(8,128)} %get-tuple-element.13), calls=%async_computation.1 | async-start | bytes 262144 | tf_op jit(solution)/shard_map/all_to_all | solution.py:305
  54.9 7.5 %all-to-all-done.1.pieces_ref = f32[16,16,128]{2,1,0:T(8,128)S(1)} async-done(((f32[16,16,128]{2,1,0:T(8,128)}), f32[16,16,128]{2,1,0:T(8,128)S(1)}, u32[]{:S(2)}, u32[]{:S(2)}) %all-to-all-start.1) | async-done | bytes 131104 | tf_op jit(solution)/shard_map/all_to_all | solution.py:305
  62.8 10.3 %all_to_all.25 = f32[16,8,128]{2,1,0:T(8,128)S(1)} all-to-all(f32[16,8,128]{2,1,0:T(8,128)S(1)} %shard_map.97), channel_id=1, replica_groups=mesh['band'=16,'grid'=16] {'grid'}, dimensions={0} | all-to-all | bytes 131072 | tf_op jit(solution)/shard_map/all_to_all | solution.py:305
  74.2 6.0 %all-to-all-start.3 = ((f32[16,128,128]{2,1,0:T(8,128)}), f32[16,128,128]{2,1,0:T(8,128)S(1)}, u32[]{:S(2)}, u32[]{:S(2)}) async-start(f32[16,128,128]{2,1,0:T(8,128)} %shard_map.98), calls=%async_computation.3 | async-start | bytes 2097152 | tf_op jit(solution)/shard_map/all_to_all | solution.py:305
  80.8 2.7 %collective-permute-start.13 = (f32[128,128]{1,0:T(8,128)S(1)}, f32[128,128]{1,0:T(8,128)S(1)}, u32[]{:S(2)}, u32[]{:S(2)}) collective-permute-start(f32[128,128]{1,0:T(8,128)S(1)} %get-tuple-element.14), channel_id=1, source_target_pairs={{0,224},{16,240},{32,192},{48,208},{64,160},{80,176},{96,128},{112... | collective-permute-start | bytes 196616 | tf_op jit(solution)/shard_map/ppermute | solution.py:309
  83.5 3.0 %collective-permute-start.10 = (f32[128,128]{1,0:T(8,128)S(1)}, f32[128,128]{1,0:T(8,128)S(1)}, u32[]{:S(2)}, u32[]{:S(2)}) collective-permute-start(f32[128,128]{1,0:T(8,128)S(1)} %get-tuple-element.14), channel_id=1, source_target_pairs={{0,128},{16,144},{32,160},{48,176},{64,192},{80,208},{96,224},{112... | collective-permute-start | bytes 196616 | tf_op jit(solution)/shard_map/ppermute | solution.py:309
  86.5 1.2 collective-permute-start.9
  87.7 22.7 %collective-permute-done.10 = f32[128,128]{1,0:T(8,128)S(1)} collective-permute-done((f32[128,128]{1,0:T(8,128)S(1)}, f32[128,128]{1,0:T(8,128)S(1)}, u32[]{:S(2)}, u32[]{:S(2)}) %collective-permute-start.10) | collective-permute-done | bytes 65568 | tf_op jit(solution)/shard_map/ppermute | solution.py:309
  110.3 1.2 collective-permute-done.8
  111.5 2.5 %collective-permute-start.12 = (f32[128,128]{1,0:T(8,128)S(1)}, f32[128,128]{1,0:T(8,128)S(1)}, u32[]{:S(2)}, u32[]{:S(2)}) collective-permute-start(f32[128,128]{1,0:T(8,128)S(1)} %collective-permute-done.10), channel_id=1, source_target_pairs={{0,64},{16,80},{32,96},{48,112},{64,0},{80,16},{96,32},{112,48},{1... | collective-permute-start | bytes 196616 | tf_op jit(solution)/shard_map/ppermute | solution.py:309
  115.9 2.6 %collective-permute-done.11 = f32[2,128,128]{2,1,0:T(8,128)S(1)} collective-permute-done((f32[2,128,128]{2,1,0:T(8,128)S(1)}, f32[2,128,128]{2,1,0:T(8,128)S(1)}, u32[]{:S(2)}, u32[]{:S(2)}) %collective-permute-start.11) | collective-permute-done | bytes 131104 | tf_op jit(solution)/shard_map/ppermute | solution.py:309
  120.7 6.1 %collective-permute-done.15 = f32[4,128,128]{2,1,0:T(8,128)S(1)} collective-permute-done((f32[4,128,128]{2,1,0:T(8,128)S(1)}, f32[4,128,128]{2,1,0:T(8,128)S(1)}, u32[]{:S(2)}, u32[]{:S(2)}) %collective-permute-start.15) | collective-permute-done | bytes 262176 | tf_op jit(solution)/shard_map/ppermute | solution.py:309
  128.0 3.8 %shard_map.100 = f32[16,2,2,8,8,128]{5,4,3,2,1,0:T(8,128)S(1)} custom-call(f32[16,2,8,8,128]{4,3,2,1,0:T(8,128)S(1)} %bitcast.40, bf16[1,8,128,128]{3,2,1,0:T(8,128)(2,1)S(1)} %copy-done.2, f32[2,8,128,128]{3,2,1,0:T(8,128)S(1)} %shard_map.99.base_ref, bf16[2,256,256]{2,1,0:T(8,128)(2,1)S(1)} %copy-done.1, bf16[2,256,256]{2,1,0:T(8,128)(2,1)S(1)} %copy-done), custom_call_target="tpu_custom_call" | custom-call | tf_op jit(solution)/shard_map/pallas_call | solution.py:405
  131.8 33.6 %all_to_all.26.pieces_ref = f32[16,256,128]{2,1,0:T(8,128)S(1)} all-to-all(f32[16,256,128]{2,1,0:T(8,128)S(1)} %bitcast.39), channel_id=1, replica_groups=mesh['band'=16,'grid'=16] {'grid'}, dimensions={0} | all-to-all | bytes 4194304 | tf_op jit(solution)/shard_map/all_to_all | solution.py:305
  165.3 1.9 %shard_map.101 = (f32[2,1,8,128,128]{4,3,2,1,0:T(8,128)}, f32[2,1,8,128,128]{4,3,2,1,0:T(8,128)}) custom-call(f32[16,256,128]{2,1,0:T(8,128)S(1)} %all_to_all.26.pieces_ref, bf16[2,256,256]{2,1,0:T(8,128)(2,1)S(1)} %copy-done.6), custom_call_target="tpu_custom_call" | custom-call | tf_op jit(solution)/shard_map/pallas_call | solution.py:418
  (60 shorter events, 9.1 us)
Async XLA Ops:
  4.8 50.1 %copy-start.1 = (bf16[2,256,256]{2,1,0:T(8,128)(2,1)S(1)}, bf16[2,256,256]{2,1,0:T(8,128)(2,1)}, u32[]{:S(2)}) copy-start(bf16[2,256,256]{2,1,0:T(8,128)(2,1)} %constant.61.clone.up_in.up_ref) | copy-start | bytes 786436
  4.8 57.6 %copy-start = (bf16[2,256,256]{2,1,0:T(8,128)(2,1)S(1)}, bf16[2,256,256]{2,1,0:T(8,128)(2,1)}, u32[]{:S(2)}) copy-start(bf16[2,256,256]{2,1,0:T(8,128)(2,1)} %constant.60.clone.down_in.down_ref) | copy-start | bytes 786436
  4.8 37.0 %all-to-all-start = ((f32[16,64,128]{2,1,0:T(8,128)}), f32[16,64,128]{2,1,0:T(8,128)S(1)}, u32[]{:S(2)}, u32[]{:S(2)}) async-start(f32[16,64,128]{2,1,0:T(8,128)} %bitcast.51), calls=%async_computation | async-start | bytes 1048576 | tf_op jit(solution)/shard_map/all_to_all | solution.py:305
  15.1 8.1 %collective-permute-start = (f32[8,64,128]{2,1,0:T(8,128)}, f32[8,64,128]{2,1,0:T(8,128)S(1)}, u32[]{:S(2)}, u32[]{:S(2)}) collective-permute-start(f32[8,64,128]{2,1,0:T(8,128)} %bitcast.60), channel_id=1, source_target_pairs={{0,16},{16,0},{32,48},{48,32},{64,80},{80,64},{96,112},{112,96},{1... | collective-permute-start | bytes 786440 | tf_op jit(solution)/shard_map/ppermute | solution.py:309
  24.2 13.8 %collective-permute-start.7 = (f32[64,128]{1,0:T(8,128)S(1)}, f32[64,128]{1,0:T(8,128)S(1)}, u32[]{:S(2)}, u32[]{:S(2)}) collective-permute-start(f32[64,128]{1,0:T(8,128)S(1)} %get-tuple-element.18), channel_id=1, source_target_pairs={{0,224},{16,240},{32,192},{48,208},{64,160},{80,176},{96,128},{112... | collective-permute-start | bytes 98312 | tf_op jit(solution)/shard_map/ppermute | solution.py:309
  27.7 10.3 %collective-permute-start.6 = (f32[64,128]{1,0:T(8,128)S(1)}, f32[64,128]{1,0:T(8,128)S(1)}, u32[]{:S(2)}, u32[]{:S(2)}) collective-permute-start(f32[64,128]{1,0:T(8,128)S(1)} %get-tuple-element.19), channel_id=1, source_target_pairs={{0,192},{16,208},{32,224},{48,240},{64,128},{80,144},{96,160},{112... | collective-permute-start | bytes 98312 | tf_op jit(solution)/shard_map/ppermute | solution.py:309
  29.5 9.0 %collective-permute-start.5 = (f32[64,128]{1,0:T(8,128)S(1)}, f32[64,128]{1,0:T(8,128)S(1)}, u32[]{:S(2)}, u32[]{:S(2)}) collective-permute-start(f32[64,128]{1,0:T(8,128)S(1)} %get-tuple-element.20), channel_id=1, source_target_pairs={{0,160},{16,176},{32,128},{48,144},{64,224},{80,240},{96,192},{112... | collective-permute-start | bytes 98312 | tf_op jit(solution)/shard_map/ppermute | solution.py:309
  34.9 6.9 %collective-permute-start.4 = (f32[64,128]{1,0:T(8,128)S(1)}, f32[64,128]{1,0:T(8,128)S(1)}, u32[]{:S(2)}, u32[]{:S(2)}) collective-permute-start(f32[64,128]{1,0:T(8,128)S(1)} %get-tuple-element.21), channel_id=1, source_target_pairs={{0,128},{16,144},{32,160},{48,176},{64,192},{80,208},{96,224},{112... | collective-permute-start | bytes 98312 | tf_op jit(solution)/shard_map/ppermute | solution.py:309
  34.9 6.9 %collective-permute-start.3 = (f32[64,128]{1,0:T(8,128)S(1)}, f32[64,128]{1,0:T(8,128)S(1)}, u32[]{:S(2)}, u32[]{:S(2)}) collective-permute-start(f32[64,128]{1,0:T(8,128)S(1)} %get-tuple-element.22), channel_id=1, source_target_pairs={{0,96},{16,112},{32,64},{48,80},{64,32},{80,48},{96,0},{112,16},{1... | collective-permute-start | bytes 98312 | tf_op jit(solution)/shard_map/ppermute | solution.py:309
  38.0 3.9 %collective-permute-start.2 = (f32[64,128]{1,0:T(8,128)S(1)}, f32[64,128]{1,0:T(8,128)S(1)}, u32[]{:S(2)}, u32[]{:S(2)}) collective-permute-start(f32[64,128]{1,0:T(8,128)S(1)} %get-tuple-element.23), channel_id=1, source_target_pairs={{0,64},{16,80},{32,96},{48,112},{64,0},{80,16},{96,32},{112,48},{1... | collective-permute-start | bytes 98312 | tf_op jit(solution)/shard_map/ppermute | solution.py:309
  38.0 3.9 %collective-permute-start.1 = (f32[64,128]{1,0:T(8,128)S(1)}, f32[64,128]{1,0:T(8,128)S(1)}, u32[]{:S(2)}, u32[]{:S(2)}) collective-permute-start(f32[64,128]{1,0:T(8,128)S(1)} %get-tuple-element.24), channel_id=1, source_target_pairs={{0,32},{16,48},{32,0},{48,16},{64,96},{80,112},{96,64},{112,80},{1... | collective-permute-start | bytes 98312 | tf_op jit(solution)/shard_map/ppermute | solution.py:309
  42.6 19.8 %all-to-all-start.1 = ((f32[16,16,128]{2,1,0:T(8,128)}), f32[16,16,128]{2,1,0:T(8,128)S(1)}, u32[]{:S(2)}, u32[]{:S(2)}) async-start(f32[16,16,128]{2,1,0:T(8,128)} %get-tuple-element.13), calls=%async_computation.1 | async-start | bytes 262144 | tf_op jit(solution)/shard_map/all_to_all | solution.py:305
  74.2 53.8 %all-to-all-start.3 = ((f32[16,128,128]{2,1,0:T(8,128)}), f32[16,128,128]{2,1,0:T(8,128)S(1)}, u32[]{:S(2)}, u32[]{:S(2)}) async-start(f32[16,128,128]{2,1,0:T(8,128)} %shard_map.98), calls=%async_computation.3 | async-start | bytes 2097152 | tf_op jit(solution)/shard_map/all_to_all | solution.py:305
  80.8 34.9 %collective-permute-start.13 = (f32[128,128]{1,0:T(8,128)S(1)}, f32[128,128]{1,0:T(8,128)S(1)}, u32[]{:S(2)}, u32[]{:S(2)}) collective-permute-start(f32[128,128]{1,0:T(8,128)S(1)} %get-tuple-element.14), channel_id=1, source_target_pairs={{0,224},{16,240},{32,192},{48,208},{64,160},{80,176},{96,128},{112... | collective-permute-start | bytes 196616 | tf_op jit(solution)/shard_map/ppermute | solution.py:309
  83.5 26.8 %collective-permute-start.10 = (f32[128,128]{1,0:T(8,128)S(1)}, f32[128,128]{1,0:T(8,128)S(1)}, u32[]{:S(2)}, u32[]{:S(2)}) collective-permute-start(f32[128,128]{1,0:T(8,128)S(1)} %get-tuple-element.14), channel_id=1, source_target_pairs={{0,128},{16,144},{32,160},{48,176},{64,192},{80,208},{96,224},{112... | collective-permute-start | bytes 196616 | tf_op jit(solution)/shard_map/ppermute | solution.py:309
  86.5 23.8 %collective-permute-start.9 = (f32[128,128]{1,0:T(8,128)S(1)}, f32[128,128]{1,0:T(8,128)S(1)}, u32[]{:S(2)}, u32[]{:S(2)}) collective-permute-start(f32[128,128]{1,0:T(8,128)S(1)} %get-tuple-element.14), channel_id=1, source_target_pairs={{0,64},{16,80},{32,96},{48,112},{64,0},{80,16},{96,32},{112,48},{1... | collective-permute-start | bytes 196616 | tf_op jit(solution)/shard_map/ppermute | solution.py:309
  87.7 23.9 %collective-permute-start.8 = (f32[128,128]{1,0:T(8,128)S(1)}, f32[128,128]{1,0:T(8,128)S(1)}, u32[]{:S(2)}, u32[]{:S(2)}) collective-permute-start(f32[128,128]{1,0:T(8,128)S(1)} %get-tuple-element.14), channel_id=1, source_target_pairs={{0,32},{16,48},{32,0},{48,16},{64,96},{80,112},{96,64},{112,80},{1... | collective-permute-start | bytes 196616 | tf_op jit(solution)/shard_map/ppermute | solution.py:309
  111.5 4.3 %collective-permute-start.12 = (f32[128,128]{1,0:T(8,128)S(1)}, f32[128,128]{1,0:T(8,128)S(1)}, u32[]{:S(2)}, u32[]{:S(2)}) collective-permute-start(f32[128,128]{1,0:T(8,128)S(1)} %collective-permute-done.10), channel_id=1, source_target_pairs={{0,64},{16,80},{32,96},{48,112},{64,0},{80,16},{96,32},{112,48},{1... | collective-permute-start | bytes 196616 | tf_op jit(solution)/shard_map/ppermute | solution.py:309
  114.0 4.4 %collective-permute-start.11 = (f32[2,128,128]{2,1,0:T(8,128)S(1)}, f32[2,128,128]{2,1,0:T(8,128)S(1)}, u32[]{:S(2)}, u32[]{:S(2)}) collective-permute-start(f32[2,128,128]{2,1,0:T(8,128)S(1)} %pad_maximum_fusion.3), channel_id=1, source_target_pairs={{0,32},{16,48},{32,0},{48,16},{64,96},{80,112},{96,64},{112,80},{1... | collective-permute-start | bytes 393224 | tf_op jit(solution)/shard_map/ppermute | solution.py:309
  114.7 12.1 %copy-start.4 = (f32[8,128,128]{2,1,0:T(8,128)S(1)}, f32[8,128,128]{2,1,0:T(8,128)}, u32[]{:S(2)}) copy-start(f32[8,128,128]{2,1,0:T(8,128)} %alda_ref.1) | copy-start | bytes 1572868
  114.7 12.2 %copy-start.5 = (f32[8,128,128]{2,1,0:T(8,128)S(1)}, f32[8,128,128]{2,1,0:T(8,128)}, u32[]{:S(2)}) copy-start(f32[8,128,128]{2,1,0:T(8,128)} %local_ref.1) | copy-start | bytes 1572868
  114.8 5.9 %collective-permute-start.14 = (f32[4,128,128]{2,1,0:T(8,128)S(1)}, f32[4,128,128]{2,1,0:T(8,128)S(1)}, u32[]{:S(2)}, u32[]{:S(2)}) collective-permute-start(f32[4,128,128]{2,1,0:T(8,128)S(1)} %pad_maximum_fusion.1), channel_id=1, source_target_pairs={{0,16},{16,0},{32,48},{48,32},{64,80},{80,64},{96,112},{112,96},{1... | collective-permute-start | bytes 786440 | tf_op jit(solution)/shard_map/ppermute | solution.py:309
  118.5 8.3 %collective-permute-start.15 = (f32[4,128,128]{2,1,0:T(8,128)S(1)}, f32[4,128,128]{2,1,0:T(8,128)S(1)}, u32[]{:S(2)}, u32[]{:S(2)}) collective-permute-start(f32[4,128,128]{2,1,0:T(8,128)S(1)} %pad_maximum_fusion.2), channel_id=1, source_target_pairs={{0,16},{16,0},{32,48},{48,32},{64,80},{80,64},{96,112},{112,96},{1... | collective-permute-start | bytes 786440 | tf_op jit(solution)/shard_map/ppermute | solution.py:309
  131.8 33.6 %copy-start.6 = (bf16[2,256,256]{2,1,0:T(8,128)(2,1)S(1)}, bf16[2,256,256]{2,1,0:T(8,128)(2,1)}, u32[]{:S(2)}) copy-start(bf16[2,256,256]{2,1,0:T(8,128)(2,1)} %constant.62.clone.x_ref) | copy-start | bytes 786436
  (2 other events, 24.3 us)
